TPU v7x, 128 devices: a whole 4x4x4 slice. The times are simulated.
128 devices in a mesh: tp: 4 (over x), dp: 32 (over z, y, core).
Axes of the slice: x: 4, y: 4, z: 4, core: 2. Of those that a mesh axis runs over, the one named last changes fastest.
Arguments:
- w_in: float32 [1, 768, 5376], P(None, None, 'tp')
- w_out: float32 [1, 3840, 768], P(None, 'tp')
- g_in: float32 [32, 1, 768, 5376], P('dp', None, None, 'tp')
- g_out: float32 [32, 1, 3840, 768], P('dp', None, 'tp')
- m_in: bfloat16 [1, 768, 5376], P(None, 'dp', 'tp')
- m_out: bfloat16 [1, 3840, 768], P(None, 'tp', 'dp')
- r_in: float32 [1, 768], P(None, 'dp')
- c_in: float32 [1, 5376], P(None, 'tp')
- r_out: float32 [1, 3840], P(None, 'tp')
- c_out: float32 [1, 768], P(None, 'dp')
- learn_rate: float32 [], replicated
- weight_decay: float32 [], replicated
- beta_two: float32 [], replicated
Outputs:
- output 1: float32 [1, 768, 5376], P(None, None, 'tp')
- output 2: float32 [1, 3840, 768], P(None, 'tp')
- output 3: bfloat16 [1, 768, 5376], P(None, 'dp', 'tp')
- output 4: bfloat16 [1, 3840, 768], P(None, 'tp', 'dp')
- output 5: float32 [1, 768], P(None, 'dp')
- output 6: float32 [1, 5376], P(None, 'tp')
- output 7: float32 [1, 3840], P(None, 'tp')
- output 8: float32 [1, 768], P(None, 'dp')
All inputs are finite; a program needn't handle non-finite values.
Results may differ from a plain program's by a relative error of at most 0.0012163.
Values sent between devices are 32-bit elements.
A program may use at most 1 GiB of HBM per device.

v0:
```python
import jax
import jax.numpy as jnp
from jax import lax
from jax.sharding import PartitionSpec as P


def local_update(weight, grad_rep, moment, row_old, col_old, learn_rate, weight_decay, beta_two, row_axis, col_axis, row_devs, col_devs):
    dp_dim = 1 if row_axis == 'dp' else 2
    grad_part = lax.psum_scatter(grad_rep[0], 'dp', scatter_dimension=dp_dim, tiled=True)
    n_rows = grad_part.shape[1] * row_devs
    n_cols = grad_part.shape[2] * col_devs
    grad_sq = grad_part * grad_part + 1e-30
    row_mean = lax.psum(jnp.sum(grad_sq, axis=2), col_axis) / n_cols
    col_mean = lax.psum(jnp.sum(grad_sq, axis=1), row_axis) / n_rows
    row_new = beta_two * row_old + (1.0 - beta_two) * row_mean
    col_new = beta_two * col_old + (1.0 - beta_two) * col_mean
    row_avg = lax.psum(jnp.sum(row_new, axis=1), row_axis) / n_rows
    second = row_new[:, :, None] * col_new[:, None, :] / row_avg[:, None, None]
    update = grad_part / jnp.sqrt(second)
    total_sq = lax.psum(jnp.sum(update * update, axis=(1, 2)), ('tp', 'dp'))
    rms_val = jnp.sqrt(total_sq / (n_rows * n_cols))
    update = update / jnp.maximum(1.0, rms_val)[:, None, None]
    mom_new = (0.9 * moment.astype(jnp.float32) + 0.1 * update).astype(jnp.bfloat16)
    width = grad_part.shape[dp_dim]
    w_block = lax.dynamic_slice_in_dim(weight, lax.axis_index('dp') * width, width, axis=dp_dim)
    w_block = w_block - learn_rate * mom_new.astype(jnp.float32) - learn_rate * weight_decay * w_block
    w_new = lax.all_gather(w_block, 'dp', axis=dp_dim, tiled=True)
    return w_new, mom_new, row_new, col_new


def solution(mesh):
    tp_devs = mesh.shape['tp']
    dp_devs = mesh.shape['dp']

    def body(w_in, w_out, g_in, g_out, m_in, m_out, r_in, c_in, r_out, c_out, learn_rate, weight_decay, beta_two):
        in_result = local_update(w_in, g_in, m_in, r_in, c_in, learn_rate, weight_decay, beta_two, 'dp', 'tp', dp_devs, tp_devs)
        out_result = local_update(w_out, g_out, m_out, r_out, c_out, learn_rate, weight_decay, beta_two, 'tp', 'dp', tp_devs, dp_devs)
        return (in_result[0], out_result[0], in_result[1], out_result[1], in_result[2], in_result[3], out_result[2], out_result[3])

    in_specs = (P(None, None, 'tp'), P(None, 'tp', None), P('dp', None, None, 'tp'), P('dp', None, 'tp', None), P(None, 'dp', 'tp'), P(None, 'tp', 'dp'), P(None, 'dp'), P(None, 'tp'), P(None, 'tp'), P(None, 'dp'), P(), P(), P())
    out_specs = (P(None, None, 'tp'), P(None, 'tp', None), P(None, 'dp', 'tp'), P(None, 'tp', 'dp'), P(None, 'dp'), P(None, 'tp'), P(None, 'tp'), P(None, 'dp'))
    return jax.shard_map(body, mesh=mesh, in_specs=in_specs, out_specs=out_specs, check_vma=False)
```

profile of v0, /device:TPU:1, one launch (start us, length us, event | category | flops | bytes accessed | tf_op | source)
XLA Modules:
  0.0 497.4 jit_solution(1021170095891714526)
XLA Ops:
  7.2 3.7 copy.30
  11.0 5.7 %copy.28 = f32[1,1,768,1344]{3,2,1,0:T(8,128)} copy(f32[1,1,768,1344]{2,3,1,0:T(8,128)} %param.15) | data formatting | bytes 8257536 | tf_op args[2]
  18.7 0.2 constant_dynamic-slice_fusion
  19.1 75.3 %reduce-scatter.6.cloned.1.call-done = f32[1,960,24]{1,2,0:T(8,128)} async-done(((f32[1,960,768]{1,2,0:T(8,128)}), f32[1,960,24]{1,2,0:T(8,128)}) %reduce-scatter.6.cloned.1.call-update) | async-done | bytes 92176 | tf_op jit(solution)/shard_map/reduce_scatter | solution.py:9
  94.4 1.0 fusion.2
  95.5 81.3 %reduce-scatter.8.cloned.1.call-done = f32[1,24,1344]{2,1,0:T(8,128)} async-done(((f32[1,768,1344]{2,1,0:T(8,128)}), f32[1,24,1344]{2,1,0:T(8,128)}) %reduce-scatter.8.cloned.1.call-update) | async-done | bytes 129040
  176.8 1.0 fusion
  177.8 8.4 %psum.56 = f32[1,24]{1,0:T(1,128)S(1)} all-reduce(f32[1,24]{1,0:T(1,128)S(1)} %bitcast.29), channel_id=1, replica_groups=mesh['tp'=4,'dp'=32] {'tp'}, use_global_device_ids=true, to_apply=%region_2.0 | all-reduce | flops 24 | bytes 192 | tf_op jit(solution)/shard_map/psum | solution.py:13
  186.3 1.3 fusion.6
  187.5 122.4 %all-reduce.2 = (f32[1]{0:T(128)}, f32[1,1344]{1,0:T(1,128)S(1)}, f32[1,960]{1,0:T(1,128)S(1)}) all-reduce(f32[1]{0:T(128)} %bitcast.6, f32[1,1344]{1,0:T(1,128)S(1)} %reduce_sum.91, f32[1,960]{1,0:T(1,128)S(1)} %bitcast.23), channel_id=1, replica_groups=mesh['tp'=4,'dp'=32] {'dp'}, use_global_device_ids=true, to_apply=%region_6.0 | all-reduce | flops 2305 | bytes 18440 | tf_op jit(solution)/shard_map/psum | solution.py:17
  310.6 0.6 fusion.4
  311.2 6.6 %all-reduce.3 = (f32[1]{0:T(128)}, f32[1,24]{1,0:T(1,128)S(1)}) all-reduce(f32[1]{0:T(128)} %bitcast.15, f32[1,24]{1,0:T(1,128)S(1)} %bitcast.28), channel_id=1, replica_groups=mesh['tp'=4,'dp'=32] {'tp'}, use_global_device_ids=true, to_apply=%region_15.0 | all-reduce | flops 25 | bytes 200 | tf_op jit(solution)/shard_map/psum | solution.py:17
  318.5 0.6 fusion.5
  319.1 1.6 multiply_reduce_fusion.1
  320.7 1.6 multiply_reduce_fusion
  322.3 68.9 %all-reduce.1 = (f32[1]{0:T(128)}, f32[1]{0:T(128)}) all-reduce(f32[1]{0:T(128)} %bitcast.8, f32[1]{0:T(128)} %bitcast.17), channel_id=1, replica_groups=mesh['tp'=4,'dp'=32] {'tp','dp'}, use_global_device_ids=true, to_apply=%region_8.0 | all-reduce | flops 2 | bytes 16 | tf_op jit(solution)/shard_map/psum | solution.py:20
  391.9 1.7 multiply_subtract_fusion.1
  393.7 2.4 constant_dynamic-slice_fusion.1
  396.1 1.3 copy.35
  398.1 1.8 multiply_subtract_fusion
  399.9 36.8 %all-gather.5.cloned.1.call-done = f32[1,960,768]{1,2,0:T(8,128)} async-done(((f32[1,960,24]{1,2,0:T(8,128)}), f32[1,960,768]{1,2,0:T(8,128)}) %all-gather.5.cloned.1.call-update) | async-done | bytes 2949136 | tf_op jit(solution)/shard_map/all_gather | solution.py:27
  436.8 3.5 copy.32
  440.2 45.0 %all-gather.3.cloned.1.call-done = f32[1,768,1344]{2,1,0:T(8,128)} async-done(((f32[1,24,1344]{2,1,0:T(8,128)}), f32[1,768,1344]{2,1,0:T(8,128)}) %all-gather.3.cloned.1.call-update) | async-done | bytes 4128784 | tf_op jit(solution)/shard_map/all_gather | solution.py:27
  485.2 5.6 %copy.31 = f32[1,768,1344]{1,2,0:T(8,128)} copy(f32[1,768,1344]{2,1,0:T(8,128)} %all-gather.3.cloned.1.call-done) | data formatting | bytes 8257536
  (25 shorter events, 0.4 us)
Async XLA Ops:
  7.2 11.5 %copy-start = (f32[1,960,768]{2,1,0:T(8,128)S(1)}, f32[1,960,768]{2,1,0:T(8,128)}, u32[]{:S(2)}) copy-start(f32[1,960,768]{2,1,0:T(8,128)} %param.14) | copy-start | bytes 8847364
  7.2 87.2 %reduce-scatter.6.cloned.1.call-start = ((), (), s32[]{:S(2)}) async-start(), calls=%async_computation.3 | async-start | bytes 3244032 | tf_op jit(solution)/shard_map/reduce_scatter | solution.py:9
  10.9 165.8 %reduce-scatter.8.cloned.1.call-start = ((), (), s32[]{:S(2)}) async-start(), calls=%async_computation.5 | async-start | bytes 4460544
  16.7 293.9 %copy-start.5 = (f32[1,960]{1,0:T(1,128)S(1)}, f32[1,960]{1,0:T(1,128)}, u32[]{:S(2)}) copy-start(f32[1,960]{1,0:T(1,128)} %param.21) | copy-start | bytes 11524
  16.7 301.8 %copy-start.2 = (f32[1,1344]{1,0:T(1,128)S(1)}, f32[1,1344]{1,0:T(1,128)}, u32[]{:S(2)}) copy-start(f32[1,1344]{1,0:T(1,128)} %param.20) | copy-start | bytes 16132
  16.7 302.4 %copy-start.6 = (f32[1,24]{1,0:T(1,128)S(1)}, f32[1,24]{1,0:T(1,128)}, u32[]{:S(2)}) copy-start(f32[1,24]{1,0:T(1,128)} %param.22) | copy-start | bytes 292
  16.7 420.1 %all-gather.5.cloned.1.call-start = ((), (), s32[]{:S(2)}) async-start(), calls=%async_computation.4 | async-start | bytes 3244032 | tf_op jit(solution)/shard_map/all_gather | solution.py:27
  187.5 252.7 %copy-start.4 = (f32[1,24]{1,0:T(1,128)}, f32[1,24]{1,0:T(1,128)S(1)}, u32[]{:S(2)}) copy-start(f32[1,24]{1,0:T(1,128)S(1)} %get-tuple-element.44) | copy-start | bytes 292
  311.2 129.0 %copy-start.1 = (f32[1,960]{1,0:T(1,128)}, f32[1,960]{1,0:T(1,128)S(1)}, u32[]{:S(2)}) copy-start(f32[1,960]{1,0:T(1,128)S(1)} %get-tuple-element.40) | copy-start | bytes 11524
  319.1 121.1 %copy-start.3 = (f32[1,24]{1,0:T(1,128)}, f32[1,24]{1,0:T(1,128)S(1)}, u32[]{:S(2)}) copy-start(f32[1,24]{1,0:T(1,128)S(1)} %multiply_add_fusion.4) | copy-start | bytes 292
  393.6 91.6 %all-gather.3.cloned.1.call-start = ((), (), s32[]{:S(2)}) async-start(), calls=%async_computation.2 | async-start | bytes 4460544 | tf_op jit(solution)/shard_map/all_gather | solution.py:27
Sparse Core Ops, SparseCore 0:
  12.2 82.1 reduce-scatter.5
  98.2 78.5 reduce-scatter.7
  393.7 42.9 all-gather.4
  439.5 45.6 all-gather.2
where the time goes:
time: 498 us; the launch traced here: 497 us
  waiting for transfers between devices  239 us (48%)
  blocking collectives  206 us (41%)
  local copies, waits for them, and re-layouts  22.6 us (5%)
  between operations  18.5 us (4%)
  other arithmetic  11.2 us (2%)
    psum x2, blocking collectives, local_update(): row_avg = lax.psum(jnp.sum(row_new, axis=1), row_axis) / n_rows  129 us
    all_gather x2, waiting for transfers between devices, local_update(): w_new = lax.all_gather(w_block, 'dp', axis=dp_dim, tiled=True)  81.8 us
    unnamed x5, waiting for transfers between devices  81.4 us
    reduce_scatter x1, waiting for transfers between devices, local_update(): lax.psum_scatter(grad_rep[0], 'dp', scatter_dimension=dp_dim, tiled=True)  75.3 us
    psum x1, blocking collectives, local_update(): total_sq = lax.psum(jnp.sum(update * update, axis=(1, 2)), ('tp', 'dp'))  68.9 us
    unnamed x20, local copies, waits for them, and re-layouts  20 us
  transfers between devices with their start and end apart: 4, of which 4 were waited for; matrix products, arithmetic and copies ran while one was open for 3% of the time, Pallas kernels for 0%

commit v1 on v0

v1 whole, which is shorter than its diff:
```python
import jax
import jax.numpy as jnp
from jax import lax
from jax.experimental import pallas as pl
from jax.experimental.pallas import tpu as pltpu
from jax.sharding import PartitionSpec as P

MESH = pl.DeviceIdType.MESH
F32 = jnp.float32
BF16 = jnp.bfloat16

D = 768
F_IN = 1344
F_OUT = 960
HALF = 1152
TAIL = 192
N_IN = 5376
N_OUT = 3840
CUT = 640
PIECES = ((0, 640), (640, 960), (960, 1152))


def half_ref(in_ref, out_ref, half, lo, hi):
    if half == 0:
        return in_ref.at[pl.ds(lo, hi - lo)]
    if hi <= F_OUT:
        return out_ref.at[pl.ds(lo, hi - lo)]
    return in_ref.at[pl.ds(lo - F_OUT + HALF, hi - lo)]


def join_tail(out_val, tail_val, pad_a, pad_b):
    pad_a[...] = jnp.zeros_like(pad_a)
    pad_b[...] = jnp.zeros_like(pad_b)
    pad_a[:, 0:64] = out_val[:, 896:960]
    pad_b[:, 0:192] = tail_val
    moved = pltpu.roll(pad_b[...], 64, 1)
    lane = lax.broadcasted_iota(jnp.int32, pad_a.shape, 1)
    mid = jnp.where(lane < 64, pad_a[...], moved[:, 0:128])
    return jnp.concatenate([out_val[:, 0:896], mid, moved[:, 128:256]], axis=1)


def kernel(scal, g_in, g_out, w_in, w_out, m_in, m_out, r_in, c_in, r_out, c_out,
           o_w_in, o_w_out, o_m_in, o_m_out, o_r_in, o_c_in, o_r_out, o_c_out,
           xown, xrecv, wown, ybuf, tbuf, t2buf, far, dirb, comb, pbuf, far2, dir2, comb2,
           mx, ms, mrecv, fo, fnew, frecv, fv, rv, qa, qb, ub, pad_a, pad_b, pad_c, pad_d, rowpad,
           load_sem, send, recv):
    x = lax.axis_index("tp")
    d = lax.axis_index("dp")
    core = lax.rem(d, 2)
    p = lax.div(d, 2)
    y = lax.rem(p, 4)
    z = lax.div(p, 4)

    def at(xx, pp, cc):
        return (xx, pp * 2 + cc)

    partner = at(x, p, 1 - core)
    sem_count = [0]
    copies = []

    def remote(src, dst, dev, sem=None):
        if sem is None:
            sem = sem_count[0]
            sem_count[0] += 1
        c = pltpu.make_async_remote_copy(src_ref=src, dst_ref=dst, send_sem=send.at[sem], recv_sem=recv.at[sem], device_id=dev, device_id_type=MESH)
        copies.append(c)
        return c

    for me in (0, 1):
        @pl.when(core == me)
        def _():
            for i, (lo, hi) in enumerate(PIECES):
                pltpu.make_async_copy(half_ref(g_in, g_out, me, lo, hi), xown.at[pl.ds(lo, hi - lo)], load_sem.at[i]).start()
            for i, (lo, hi) in enumerate(PIECES):
                pltpu.make_async_copy(half_ref(w_in, w_out, me, lo, hi), wown.at[pl.ds(lo, hi - lo)], load_sem.at[3 + i]).start()

    barrier = pltpu.get_barrier_semaphore()
    greet = [at(x, z * 4 + lax.rem(y + 1, 4), core), at(x, z * 4 + lax.rem(y + 3, 4), core),
             at(x, lax.rem(z + 1, 4) * 4 + y, core), at(x, lax.rem(z + 3, 4) * 4 + y, core)]
    line = []
    for k in range(1, 8):
        other = lax.rem(x * 2 + core + k, 8)
        line.append(at(lax.div(other, 2), p, lax.rem(other, 2)))
    plane = [at(x, lax.rem(p + k, 16), core) for k in range(1, 16)]
    for dev in greet + line:
        pl.semaphore_signal(barrier, inc=1, device_id=dev, device_id_type=MESH)
    pl.semaphore_wait(barrier, len(greet) + len(line))

    swap = []
    for i, (lo, hi) in enumerate(PIECES):
        sem = sem_count[0]
        sem_count[0] += 1
        swap.append(sem)
        for me in (0, 1):
            @pl.when(core == me)
            def _():
                pltpu.make_async_remote_copy(
                    src_ref=half_ref(g_in, g_out, 1 - me, lo, hi), dst_ref=xrecv.at[pl.ds(lo, hi - lo)],
                    send_sem=send.at[sem], recv_sem=recv.at[sem], device_id=partner, device_id_type=MESH).start()

    first = m_in[:, 0:HALF].astype(F32)
    second = join_tail(m_out[...].astype(F32), m_in[:, HALF:F_IN].astype(F32), pad_a, pad_b)
    on_first = core == 0
    mx[core] = jnp.where(on_first, first, second)
    ms[...] = jnp.where(on_first, second, first)
    m_copy = remote(ms, mx.at[core], partner)
    m_copy.start()
    fo[...] = jnp.where(on_first, c_in[:, 0:HALF], join_tail(r_out[...], c_in[:, HALF:F_IN], pad_c, pad_d))

    def transpose_in(j, _):
        rows = pl.ds(pl.multiple_of(j * 128, 128), 128)
        for h in range(2):
            cols = pl.ds(h * 384, 384)
            t = (xown[rows, cols] + xrecv[rows, cols]).T
            for i in range(16):
                tbuf[2 * h + i // 8, (i // 2) % 4, i % 2, :, rows] = t[24 * i:24 * i + 24]
        return 0

    def swap_wait(i):
        lo, hi = PIECES[i]
        pltpu.make_async_copy(xown.at[pl.ds(lo, hi - lo)], xown.at[pl.ds(lo, hi - lo)], load_sem.at[i]).wait()
        pltpu.make_async_remote_copy(
            src_ref=xown.at[pl.ds(lo, hi - lo)], dst_ref=xrecv.at[pl.ds(lo, hi - lo)],
            send_sem=send.at[swap[i]], recv_sem=recv.at[swap[i]], device_id=partner, device_id_type=MESH).wait_recv()

    part_a, part_b = pl.ds(0, CUT), pl.ds(CUT, HALF - CUT)
    ring = ((y, at(x, z * 4 + lax.rem(y + 1, 4), core), at(x, z * 4 + lax.rem(y + 3, 4), core)),
            (z, at(x, lax.rem(z + 1, 4) * 4 + y, core), at(x, lax.rem(z + 3, 4) * 4 + y, core)))

    def chunk(buf, a, k, lanes):
        return buf.at[:, k, 0, :, lanes] if a == 0 else buf.at[k, :, 1, :, lanes]

    swap_wait(0)
    lax.fori_loop(0, 5, transpose_in, 0)
    ph = []
    for a in range(2):
        i, right, left = ring[a]
        r, l, f = lax.rem(i + 1, 4), lax.rem(i + 3, 4), lax.rem(i + 2, 4)
        far_a = remote(chunk(tbuf, a, f, part_a), far.at[a, :, :, part_a], right)
        dir_a = remote(chunk(tbuf, a, l, part_a), dirb.at[a, :, :, part_a], left)
        far_b = remote(chunk(tbuf, a, f, part_b), far.at[a, :, :, part_b], left)
        dir_b = remote(chunk(tbuf, a, r, part_b), dirb.at[a, :, :, part_b], right)
        comb_a = remote(chunk(tbuf, a, r, part_a), comb.at[a, :, :, part_a], right)
        comb_b = remote(chunk(tbuf, a, l, part_b), comb.at[a, :, :, part_b], left)
        ph.append((i, r, l, far_a, dir_a, far_b, dir_b, comb_a, comb_b))
        far_a.start()
        dir_a.start()
    swap_wait(1)
    swap_wait(2)
    lax.fori_loop(5, 9, transpose_in, 0)
    for a in range(2):
        ph[a][5].start()
        ph[a][6].start()
    for which, lanes in ((0, part_a), (1, part_b)):
        for a in range(2):
            i, r, l, far_a, dir_a, far_b, dir_b, comb_a, comb_b = ph[a]
            k = (r, l)[which]
            (far_a, far_b)[which].wait_recv()
            for q in range(4):
                if a == 0:
                    tbuf[q, k, 0, :, lanes] += far[a, q, :, lanes]
                else:
                    tbuf[k, q, 1, :, lanes] += far[a, q, :, lanes]
            (comb_a, comb_b)[which].start()
    for a in range(2):
        i, r, l, far_a, dir_a, far_b, dir_b, comb_a, comb_b = ph[a]
        for c in (dir_a, dir_b, comb_a, comb_b):
            c.wait_recv()
        for q in range(4):
            mine = tbuf[q, i, 0] if a == 0 else tbuf[i, q, 1]
            pbuf[a, q] = mine + dirb[a, q] + comb[a, q]

    ph = []
    for a in range(2):
        i, right, left = ring[1 - a]
        r, l, f = lax.rem(i + 1, 4), lax.rem(i + 3, 4), lax.rem(i + 2, 4)
        far_a = remote(pbuf.at[a, f, :, part_a], far2.at[a, :, part_a], right)
        far_b = remote(pbuf.at[a, f, :, part_b], far2.at[a, :, part_b], left)
        dir_a = remote(pbuf.at[a, l, :, part_a], dir2.at[a, :, part_a], left)
        dir_b = remote(pbuf.at[a, r, :, part_b], dir2.at[a, :, part_b], right)
        comb_a = remote(pbuf.at[a, r, :, part_a], comb2.at[a, :, part_a], right)
        comb_b = remote(pbuf.at[a, l, :, part_b], comb2.at[a, :, part_b], left)
        for c in (far_a, far_b, dir_a, dir_b):
            c.start()
        ph.append((i, r, l, far_a, dir_a, far_b, dir_b, comb_a, comb_b))
    for which, lanes in ((0, part_a), (1, part_b)):
        for a in range(2):
            i, r, l, far_a, dir_a, far_b, dir_b, comb_a, comb_b = ph[a]
            (far_a, far_b)[which].wait_recv()
            pbuf[a, (r, l)[which], :, lanes] += far2[a, :, lanes]
            (comb_a, comb_b)[which].start()
    parts = []
    for a in range(2):
        i, r, l, far_a, dir_a, far_b, dir_b, comb_a, comb_b = ph[a]
        for c in (dir_a, dir_b, comb_a, comb_b):
            c.wait_recv()
        parts.append(pbuf[a, i] + dir2[a] + comb2[a])

    lane = lax.broadcasted_iota(jnp.int32, (1, HALF), 1)
    is_in = lane >= jnp.where(on_first, 0, F_OUT)
    eye = lax.broadcasted_iota(jnp.int32, (48, 128), 0) == lax.broadcasted_iota(jnp.int32, (48, 128), 1)

    def to_row(col):
        return jnp.sum(jnp.where(eye, col, 0.0), axis=0, keepdims=True)

    def to_col(row):
        return jnp.sum(jnp.where(eye, row, 0.0), axis=1, keepdims=True)

    g = jnp.concatenate(parts, axis=0)
    sq = g * g + 1e-30
    fv[p] = jnp.sum(sq, axis=0, keepdims=True)
    fv_copies = [remote(fv.at[p], fv.at[p], dev) for dev in plane]
    for c in fv_copies:
        c.start()
    rv[x, core] = jnp.zeros((8, 128), F32)
    rv[x, core, 0:1, :] = to_row(jnp.sum(jnp.where(is_in, sq, 0.0), axis=1, keepdims=True))
    rv[x, core, 1:2, :] = to_row(jnp.sum(jnp.where(is_in, 0.0, sq), axis=1, keepdims=True))
    for row, ref in ((2, r_in), (3, c_out)):
        rowpad[...] = jnp.zeros_like(rowpad)
        rowpad[0:1, 0:24] = ref[...]
        rv[x, core, row:row + 1, :] = jnp.where(on_first, rowpad[...], pltpu.roll(rowpad[...], 24, 1))[0:1]
    rv_copies = [remote(rv.at[x, core], rv.at[x, core], dev) for dev in line]
    for c in rv_copies:
        c.start()

    lr, wd, beta = scal[0], scal[1], scal[2]
    for c in rv_copies:
        c.wait_recv()
    row_sum = jnp.sum(rv[...].reshape(8, 8, 128), axis=0)
    row_old = rv[0, 0] + rv[0, 1]
    r_new = beta * row_old[2:3] + (1.0 - beta) * (row_sum[0:1] / N_IN)
    c_new = beta * row_old[3:4] + (1.0 - beta) * (row_sum[1:2] / N_OUT)
    row_scale_in = 1.0 / jnp.sqrt(to_col(r_new))
    row_scale_out = 1.0 / jnp.sqrt(to_col(c_new))
    for c in fv_copies:
        c.wait_recv()
    f_new = beta * fo[...] + (1.0 - beta) * (jnp.sum(fv[...], axis=0) / D)
    fnew[...] = f_new
    f_copy = remote(fnew, frecv, partner)
    f_copy.start()
    u = g * jnp.where(is_in, row_scale_in, row_scale_out) * (1.0 / jnp.sqrt(f_new))
    ub[...] = u
    uu = u * u

    def total(v):
        return jnp.sum(jnp.sum(v, axis=0, keepdims=True), axis=1, keepdims=True)

    sum_rows = jnp.sum(r_new, axis=1, keepdims=True)
    qa[x, core] = jnp.zeros((8, 128), F32)
    qa[x, core, 0:1, :] = jnp.broadcast_to(total(jnp.where(is_in, uu, 0.0)), (1, 128))
    qa[x, core, 1:2, :] = jnp.broadcast_to(total(jnp.where(is_in, 0.0, uu)), (1, 128))
    qa[x, core, 2:3, :] = jnp.broadcast_to(total(jnp.where(is_in, 0.0, f_new)), (1, 128))
    qa_copies = [remote(qa.at[x, core], qa.at[x, core], dev) for dev in line]
    for c in qa_copies:
        c.start()
    for c in qa_copies:
        c.wait_recv()
    line_sum = jnp.sum(qa[...].reshape(8, 8, 128), axis=0)
    qb[p] = line_sum
    qb[p, 3:4, :] = jnp.broadcast_to(sum_rows, (1, 128))
    qb_copies = [remote(qb.at[p], qb.at[p], dev) for dev in plane]
    for c in qb_copies:
        c.start()
    for c in qb_copies:
        c.wait_recv()
    plane_sum = jnp.sum(qb[...], axis=0)
    mean_in = plane_sum[3:4, 0:1] / D
    mean_out = line_sum[2:3, 0:1] / N_OUT
    rms_in = jnp.sqrt(plane_sum[0:1, 0:1] * mean_in / (D * N_IN))
    rms_out = jnp.sqrt(plane_sum[1:2, 0:1] * mean_out / (D * N_OUT))
    scale = jnp.where(is_in, jnp.sqrt(mean_in) / jnp.maximum(1.0, rms_in), jnp.sqrt(mean_out) / jnp.maximum(1.0, rms_out))

    m_copy.wait_recv()
    for a in range(2):
        upd = ub[24 * a:24 * a + 24, :] * scale
        t2buf[z, y, a] = (0.9 * mx[a] + 0.1 * upd).astype(BF16).astype(F32)

    def chunk_one(a, k, lanes):
        return t2buf.at[k, y, 0, :, lanes] if a == 0 else t2buf.at[z, k, 1, :, lanes]

    def gather(ref, ring_of):
        fwd = []
        for a in range(2):
            i, right, left = ring_of[a]
            r, l = lax.rem(i + 1, 4), lax.rem(i + 3, 4)
            ra = remote(ref(a, i, part_a), ref(a, i, part_a), right)
            lb = remote(ref(a, i, part_b), ref(a, i, part_b), left)
            rb = remote(ref(a, i, part_b), ref(a, i, part_b), right)
            la = remote(ref(a, i, part_a), ref(a, i, part_a), left)
            for c in (ra, lb, rb, la):
                c.start()
            fa = remote(ref(a, l, part_a), ref(a, l, part_a), right)
            fb = remote(ref(a, r, part_b), ref(a, r, part_b), left)
            fwd.append((ra, lb, rb, la, fa, fb))
        for n in range(2):
            for a in range(2):
                fwd[a][n].wait_recv()
                fwd[a][4 + n].start()
        return [c for a in range(2) for c in fwd[a][2:]]

    pending = gather(chunk_one, (ring[1], ring[0]))
    mo_copy = remote(t2buf.at[z, y, 1 - core], mrecv, partner)
    mo_copy.start()
    for c in pending:
        c.wait_recv()
    pending = gather(lambda a, k, lanes: chunk(t2buf, a, k, lanes), ring)

    mo_copy.wait_recv()
    f_copy.wait_recv()
    for mine, theirs, out_in, out_out in ((t2buf[z, y, core], mrecv[...], o_m_in, o_m_out), (f_new, frecv[...], o_c_in, o_r_out)):
        lo = jnp.where(on_first, mine, theirs)
        hi = jnp.where(on_first, theirs, mine)
        out_in[:, 0:HALF] = lo.astype(out_in.dtype)
        out_out[...] = hi[:, 0:F_OUT].astype(out_out.dtype)
        out_in[:, HALF:F_IN] = pltpu.roll(hi[:, 896:1152], 192, 1)[:, 0:TAIL].astype(out_in.dtype)
    for new, out in ((r_new, o_r_in), (c_new, o_c_out)):
        rowpad[...] = jnp.broadcast_to(new, (8, 128))
        out[...] = jnp.where(on_first, rowpad[...], pltpu.roll(rowpad[...], 104, 1))[0:1, 0:24]

    for c in pending:
        c.wait_recv()

    for i, (lo, hi) in enumerate(PIECES):
        pltpu.make_async_copy(wown.at[pl.ds(lo, hi - lo)], wown.at[pl.ds(lo, hi - lo)], load_sem.at[3 + i]).wait()
    lr_wd = lr * wd

    def transpose_out(j, _):
        rows = pl.ds(pl.multiple_of(j * 128, 128), 128)
        for h in range(2):
            cols = pl.ds(h * 384, 384)
            t = jnp.concatenate([t2buf[2 * h + i // 8, (i // 2) % 4, i % 2, :, rows] for i in range(16)], axis=0)
            w = wown[rows, cols]
            ybuf[rows, cols] = w - lr * t.T - lr_wd * w
        return 0

    out_sems = []
    for i, (lo, hi) in enumerate(PIECES):
        sem = sem_count[0]
        sem_count[0] += 1
        out_sems.append(sem)
        lax.fori_loop((0, 5, 8)[i], (5, 8, 9)[i], transpose_out, 0)
        for me in (0, 1):
            @pl.when(core == me)
            def _():
                src = ybuf.at[pl.ds(lo, hi - lo)]
                dst = half_ref(o_w_in, o_w_out, me, lo, hi)
                pltpu.make_async_remote_copy(src_ref=src, dst_ref=dst, send_sem=send.at[sem], recv_sem=recv.at[sem], device_id=partner, device_id_type=MESH).start()
                pltpu.make_async_copy(src, dst, load_sem.at[6 + i]).start()

    for c in copies:
        c.wait_send()
    for i, (lo, hi) in enumerate(PIECES):
        for me in (0, 1):
            @pl.when(core == me)
            def _():
                src = ybuf.at[pl.ds(lo, hi - lo)]
                mine = half_ref(o_w_in, o_w_out, me, lo, hi)
                theirs = half_ref(o_w_in, o_w_out, 1 - me, lo, hi)
                pltpu.make_async_copy(src, mine, load_sem.at[6 + i]).wait()
                out = pltpu.make_async_remote_copy(src_ref=src, dst_ref=theirs, send_sem=send.at[out_sems[i]], recv_sem=recv.at[out_sems[i]], device_id=partner, device_id_type=MESH)
                out.wait_send()
                out.wait_recv()
                pltpu.make_async_remote_copy(
                    src_ref=half_ref(g_in, g_out, 1 - me, lo, hi), dst_ref=xrecv.at[pl.ds(lo, hi - lo)],
                    send_sem=send.at[swap[i]], recv_sem=recv.at[swap[i]], device_id=partner, device_id_type=MESH).wait_send()
    assert sem_count[0] == N_SEMS, sem_count[0]


N_SEMS = 3 + 1 + 12 + 12 + 15 + 7 + 1 + 7 + 15 + 12 + 1 + 12 + 3


def call(*args):
    vmem = pl.BlockSpec(memory_space=pltpu.VMEM)
    hbm = pl.BlockSpec(memory_space=pl.ANY)
    smem = pl.BlockSpec(memory_space=pltpu.SMEM)
    sds = jax.ShapeDtypeStruct
    return pl.pallas_call(
        kernel,
        name="adafactor_step",
        out_shape=(sds((F_IN, D), F32), sds((F_OUT, D), F32), sds((24, F_IN), BF16), sds((24, F_OUT), BF16),
                   sds((1, 24), F32), sds((1, F_IN), F32), sds((1, F_OUT), F32), sds((1, 24), F32)),
        in_specs=[smem] + [hbm] * 4 + [vmem] * 6,
        out_specs=(hbm, hbm) + (vmem,) * 6,
        scratch_shapes=[
            pltpu.VMEM((HALF, D), F32), pltpu.VMEM((HALF, D), F32), pltpu.VMEM((HALF, D), F32), pltpu.VMEM((HALF, D), F32),
            pltpu.VMEM((4, 4, 2, 24, HALF), F32), pltpu.VMEM((4, 4, 2, 24, HALF), F32),
            pltpu.VMEM((2, 4, 24, HALF), F32), pltpu.VMEM((2, 4, 24, HALF), F32), pltpu.VMEM((2, 4, 24, HALF), F32), pltpu.VMEM((2, 4, 24, HALF), F32),
            pltpu.VMEM((2, 24, HALF), F32), pltpu.VMEM((2, 24, HALF), F32), pltpu.VMEM((2, 24, HALF), F32),
            pltpu.VMEM((2, 24, HALF), F32), pltpu.VMEM((24, HALF), F32), pltpu.VMEM((24, HALF), F32),
            pltpu.VMEM((1, HALF), F32), pltpu.VMEM((1, HALF), F32), pltpu.VMEM((1, HALF), F32),
            pltpu.VMEM((16, 1, HALF), F32), pltpu.VMEM((4, 2, 8, 128), F32), pltpu.VMEM((4, 2, 8, 128), F32), pltpu.VMEM((16, 8, 128), F32),
            pltpu.VMEM((48, HALF), F32), pltpu.VMEM((24, 128), F32), pltpu.VMEM((24, 256), F32), pltpu.VMEM((1, 128), F32), pltpu.VMEM((1, 256), F32), pltpu.VMEM((8, 128), F32),
            pltpu.SemaphoreType.DMA((9,)), pltpu.SemaphoreType.DMA((N_SEMS,)), pltpu.SemaphoreType.DMA((N_SEMS,)),
        ],
        compiler_params=pltpu.CompilerParams(collective_id=0, has_side_effects=True, vmem_limit_bytes=48 * 1024 * 1024),
    )(*args)


def solution(mesh):
    def body(w_in, w_out, g_in, g_out, m_in, m_out, r_in, c_in, r_out, c_out, learn_rate, weight_decay, beta_two):
        scal = jnp.stack([learn_rate, weight_decay, beta_two])
        outs = call(scal, g_in[0, 0].T, g_out[0, 0], w_in[0].T, w_out[0], m_in[0], m_out[0].T, r_in, c_in, r_out, c_out)
        return (outs[0].T[None], outs[1][None], outs[2][None], outs[3].T[None], outs[4], outs[5], outs[6], outs[7])

    in_specs = (P(None, None, 'tp'), P(None, 'tp', None), P('dp', None, None, 'tp'), P('dp', None, 'tp', None), P(None, 'dp', 'tp'), P(None, 'tp', 'dp'), P(None, 'dp'), P(None, 'tp'), P(None, 'tp'), P(None, 'dp'), P(), P(), P())
    out_specs = (P(None, None, 'tp'), P(None, 'tp', None), P(None, 'dp', 'tp'), P(None, 'tp', 'dp'), P(None, 'dp'), P(None, 'tp'), P(None, 'tp'), P(None, 'dp'))
    return jax.shard_map(body, mesh=mesh, in_specs=in_specs, out_specs=out_specs, check_vma=False)
```

time: 498 us -> 103 us (0.21)
  waiting for transfers between devices: 239 us -> 0 us
  blocking collectives: 206 us -> 0 us
  Pallas kernels: 0 us -> 83.9 us
  between operations: 18.5 us -> 2.59 us
  other arithmetic: 11.2 us -> 0.08 us
  local copies, waits for them, and re-layouts: 22.6 us -> 15.7 us
    psum x4 -> x0, blocking collectives: 206 us -> none  [the longest x2 129 us: local_update(): row_avg = lax.psum(jnp.sum(row_new, axis=1), row_axis) / n_rows]
    pallas_call x0 -> x1, Pallas kernels: none -> 83.9 us  [call(): pl.pallas_call(kernel, name='adafactor_step', out_shape=(sds((F_IN, D), F...]
    all_gather x2 -> x0, waiting for transfers between devices: 81.8 us -> none  [local_update(): w_new = lax.all_gather(w_block, 'dp', axis=dp_dim, tiled=True)]
    unnamed x5 -> x0, waiting for transfers between devices: 81.4 us -> none
    reduce_scatter x1 -> x0, waiting for transfers between devices: 75.3 us -> none  [local_update(): lax.psum_scatter(grad_rep[0], 'dp', scatter_dimension=dp_dim, tiled=True)]
    reduce_sum x6 -> x0, other arithmetic: 7.17 us -> none  [the longest x2 3.23 us: local_update(): total_sq = lax.psum(jnp.sum(update * update, axis=(1, 2)), ('tp', 'dp'))]
    unnamed x20 -> x22, local copies, waits for them, and re-layouts: 20 us -> 15.7 us
  transfers between devices with their start and end apart: 4 -> 0, of which waited for: 4 -> 0; matrix products, arithmetic and copies ran while one was open for 3% -> 0% of each run, Pallas kernels for 0% -> 0%
where the time goes in v1:
time: 103 us; the launch traced here: 102 us
  Pallas kernels  83.9 us (81%)
  local copies, waits for them, and re-layouts  15.7 us (15%)
  between operations  2.59 us (3%)
    pallas_call x1, Pallas kernels, call(): pl.pallas_call(kernel, name='adafactor_step', out_shape=(sds((F_IN, D), F...  83.9 us
    unnamed x22, local copies, waits for them, and re-layouts  15.7 us

profile of v1, /device:TPU:1, one launch (start us, length us, event | category | flops | bytes accessed | tf_op | source)
XLA Modules:
  0.0 102.3 jit_solution(1548737820361981689)
XLA Ops:
  2.6 0.1 pad_maximum_fusion.scal
  2.6 0.0 copy-start
  2.6 1.8 %copy-done = f32[1,1,960,768]{3,2,1,0:T(8,128)S(1)} copy-done((f32[1,1,960,768]{3,2,1,0:T(8,128)S(1)}, f32[1,1,960,768]{3,2,1,0:T(8,128)}, u32[]{:S(2)}) %copy-start) | copy-done | bytes 2949144
  4.5 0.0 copy-start.1
  4.5 0.9 copy-done.1
  5.4 0.0 copy-start.2
  5.4 0.8 copy-done.2
  6.2 0.0 copy-start.3
  6.2 0.7 copy-done.3
  6.9 0.0 copy-start.4
  6.9 0.7 copy-done.4
  7.5 0.0 copy-start.5
  7.5 0.7 copy-done.5
  8.2 0.0 copy-start.6
  8.2 0.7 copy-done.6
  8.9 83.9 %adafactor_step.1 = (f32[1344,768]{1,0:T(8,128)}, f32[960,768]{1,0:T(8,128)S(1)}, bf16[24,1344]{1,0:T(8,128)(2,1)S(1)}, bf16[24,960]{1,0:T(8,128)(2,1)S(1)}, f32...) custom-call(f32[3]{0:T(128)S(1)} %pad_maximum_fusion.scal, ...), custom_call_target="tpu_custom_call" | custom-call | tf_op jit(solution)/shard_map/adafactor_step/pallas_call | solution.py:377
  92.8 4.4 %copy.32 = f32[1,768,1344]{1,2,0:T(8,128)} copy(f32[1,768,1344]{1,2,0:T(8,128)} %bitcast.34) | data formatting | bytes 8257536
  97.2 1.6 %copy.33 = f32[1,960,768]{2,1,0:T(8,128)} copy(f32[1,960,768]{2,1,0:T(8,128)S(1)} %bitcast.27) | data formatting | bytes 5898240
  98.8 0.6 copy.34
  99.4 0.6 copy.35
  100.1 0.5 copy.36
  100.6 0.6 copy.37
  101.2 0.6 copy.38
  101.8 0.5 copy.39
Async XLA Ops:
  2.6 1.8 %copy-start = (f32[1,1,960,768]{3,2,1,0:T(8,128)S(1)}, f32[1,1,960,768]{3,2,1,0:T(8,128)}, u32[]{:S(2)}) copy-start(f32[1,1,960,768]{3,2,1,0:T(8,128)} %param.16) | copy-start | bytes 8847364
  4.5 0.9 copy-start.1
  5.4 0.8 copy-start.2
  6.2 0.7 copy-start.3
  6.9 0.7 copy-start.4
  7.5 0.7 copy-start.5
  8.2 0.7 copy-start.6

commit v2 on v1

--- a/solution.py
+++ b/solution.py
@@ -39,9 +39,10 @@
     return jnp.concatenate([out_val[:, 0:896], mid, moved[:, 128:256]], axis=1)
 
 
-def kernel(scal, g_in, g_out, w_in, w_out, m_in, m_out, r_in, c_in, r_out, c_out,
-           o_w_in, o_w_out, o_m_in, o_m_out, o_r_in, o_c_in, o_r_out, o_c_out,
-           xown, xrecv, wown, ybuf, tbuf, t2buf, far, dirb, comb, pbuf, far2, dir2, comb2,
+def kernel(lr_ref, wd_ref, beta_ref, g_in, g_out, w_in, w_out, h_m_in, h_m_out, h_r_in, h_c_in, h_r_out, h_c_out,
+           o_w, o_m_in, o_m_out, o_r_in, o_c_in, o_r_out, o_c_out,
+           m_in, m_out, r_in, c_in, r_out, c_out,
+           xown, xrecv, wown, tbuf, t2buf, far, dirb, comb, pbuf, far2, dir2, comb2,
            mx, ms, mrecv, fo, fnew, frecv, fv, rv, qa, qb, ub, pad_a, pad_b, pad_c, pad_d, rowpad,
            load_sem, send, recv):
     x = lax.axis_index("tp")
@@ -73,6 +74,11 @@
                 pltpu.make_async_copy(half_ref(g_in, g_out, me, lo, hi), xown.at[pl.ds(lo, hi - lo)], load_sem.at[i]).start()
             for i, (lo, hi) in enumerate(PIECES):
                 pltpu.make_async_copy(half_ref(w_in, w_out, me, lo, hi), wown.at[pl.ds(lo, hi - lo)], load_sem.at[3 + i]).start()
+
+    small = [pltpu.make_async_copy(src, dst, load_sem.at[6 + n]) for n, (src, dst) in enumerate((
+        (h_m_in, m_in), (h_m_out, m_out), (h_r_in, r_in), (h_c_in, c_in), (h_r_out, r_out), (h_c_out, c_out)))]
+    for c in small:
+        c.start()
 
     barrier = pltpu.get_barrier_semaphore()
     greet = [at(x, z * 4 + lax.rem(y + 1, 4), core), at(x, z * 4 + lax.rem(y + 3, 4), core),
@@ -98,6 +104,8 @@
                     src_ref=half_ref(g_in, g_out, 1 - me, lo, hi), dst_ref=xrecv.at[pl.ds(lo, hi - lo)],
                     send_sem=send.at[sem], recv_sem=recv.at[sem], device_id=partner, device_id_type=MESH).start()
 
+    for c in small:
+        c.wait()
     first = m_in[:, 0:HALF].astype(F32)
     second = join_tail(m_out[...].astype(F32), m_in[:, HALF:F_IN].astype(F32), pad_a, pad_b)
     on_first = core == 0
@@ -223,7 +231,7 @@
     for c in rv_copies:
         c.start()
 
-    lr, wd, beta = scal[0], scal[1], scal[2]
+    lr, wd, beta = lr_ref[0], wd_ref[0], beta_ref[0]
     for c in rv_copies:
         c.wait_recv()
     row_sum = jnp.sum(rv[...].reshape(8, 8, 128), axis=0)
@@ -324,65 +332,65 @@
         pltpu.make_async_copy(wown.at[pl.ds(lo, hi - lo)], wown.at[pl.ds(lo, hi - lo)], load_sem.at[3 + i]).wait()
     lr_wd = lr * wd
 
+    base = core * HALF
+
     def transpose_out(j, _):
         rows = pl.ds(pl.multiple_of(j * 128, 128), 128)
+        dest = pl.ds(pl.multiple_of(base + j * 128, 128), 128)
         for h in range(2):
             cols = pl.ds(h * 384, 384)
             t = jnp.concatenate([t2buf[2 * h + i // 8, (i // 2) % 4, i % 2, :, rows] for i in range(16)], axis=0)
             w = wown[rows, cols]
-            ybuf[rows, cols] = w - lr * t.T - lr_wd * w
+            o_w[dest, cols] = w - lr * t.T - lr_wd * w
         return 0
 
-    out_sems = []
-    for i, (lo, hi) in enumerate(PIECES):
-        sem = sem_count[0]
-        sem_count[0] += 1
-        out_sems.append(sem)
-        lax.fori_loop((0, 5, 8)[i], (5, 8, 9)[i], transpose_out, 0)
-        for me in (0, 1):
-            @pl.when(core == me)
-            def _():
-                src = ybuf.at[pl.ds(lo, hi - lo)]
-                dst = half_ref(o_w_in, o_w_out, me, lo, hi)
-                pltpu.make_async_remote_copy(src_ref=src, dst_ref=dst, send_sem=send.at[sem], recv_sem=recv.at[sem], device_id=partner, device_id_type=MESH).start()
-                pltpu.make_async_copy(src, dst, load_sem.at[6 + i]).start()
-
+    out_copies = []
+    for j0, j1 in ((0, 3), (3, 6), (6, 9)):
+        lax.fori_loop(j0, j1, transpose_out, 0)
+        span = pl.ds(pl.multiple_of(base + j0 * 128, 128), (j1 - j0) * 128)
+        c = remote(o_w.at[span], o_w.at[span], partner)
+        c.start()
+        out_copies.append(c)
+    for c in out_copies:
+        c.wait_recv()
     for c in copies:
         c.wait_send()
     for i, (lo, hi) in enumerate(PIECES):
-        for me in (0, 1):
-            @pl.when(core == me)
-            def _():
-                src = ybuf.at[pl.ds(lo, hi - lo)]
-                mine = half_ref(o_w_in, o_w_out, me, lo, hi)
-                theirs = half_ref(o_w_in, o_w_out, 1 - me, lo, hi)
-                pltpu.make_async_copy(src, mine, load_sem.at[6 + i]).wait()
-                out = pltpu.make_async_remote_copy(src_ref=src, dst_ref=theirs, send_sem=send.at[out_sems[i]], recv_sem=recv.at[out_sems[i]], device_id=partner, device_id_type=MESH)
-                out.wait_send()
-                out.wait_recv()
-                pltpu.make_async_remote_copy(
-                    src_ref=half_ref(g_in, g_out, 1 - me, lo, hi), dst_ref=xrecv.at[pl.ds(lo, hi - lo)],
-                    send_sem=send.at[swap[i]], recv_sem=recv.at[swap[i]], device_id=partner, device_id_type=MESH).wait_send()
+        pltpu.make_async_remote_copy(
+            src_ref=xown.at[pl.ds(lo, hi - lo)], dst_ref=xrecv.at[pl.ds(lo, hi - lo)],
+            send_sem=send.at[swap[i]], recv_sem=recv.at[swap[i]], device_id=partner, device_id_type=MESH).wait_send()
     assert sem_count[0] == N_SEMS, sem_count[0]
 
 
 N_SEMS = 3 + 1 + 12 + 12 + 15 + 7 + 1 + 7 + 15 + 12 + 1 + 12 + 3
+
+
+def store_kernel(w, m_in, m_out, r_in, c_in, r_out, c_out, o_w_in, o_w_out, o_m_in, o_m_out, o_r_in, o_c_in, o_r_out, o_c_out, sem):
+    pairs = [(w.at[pl.ds(0, HALF)], o_w_in.at[pl.ds(0, HALF)]), (w.at[pl.ds(HALF, F_OUT)], o_w_out), (w.at[pl.ds(HALF + F_OUT, TAIL)], o_w_in.at[pl.ds(HALF, TAIL)]),
+             (m_in, o_m_in), (m_out, o_m_out), (r_in, o_r_in), (c_in, o_c_in), (r_out, o_r_out), (c_out, o_c_out)]
+    work = [pltpu.make_async_copy(src, dst, sem.at[n]) for n, (src, dst) in enumerate(pairs)]
+    for c in work:
+        c.start()
+    for c in work:
+        c.wait()
 
 
 def call(*args):
     vmem = pl.BlockSpec(memory_space=pltpu.VMEM)
-    hbm = pl.BlockSpec(memory_space=pl.ANY)
+    hbm = pl.BlockSpec(memory_space=pltpu.HBM)
     smem = pl.BlockSpec(memory_space=pltpu.SMEM)
     sds = jax.ShapeDtypeStruct
-    return pl.pallas_call(
+    small = (((24, F_IN), BF16), ((24, F_OUT), BF16), ((1, 24), F32), ((1, F_IN), F32), ((1, F_OUT), F32), ((1, 24), F32))
+    args = args[:3] + tuple(pltpu.with_memory_space_constraint(a, pltpu.HBM) for a in args[3:])
+    held = pl.pallas_call(
         kernel,
         name="adafactor_step",
-        out_shape=(sds((F_IN, D), F32), sds((F_OUT, D), F32), sds((24, F_IN), BF16), sds((24, F_OUT), BF16),
-                   sds((1, 24), F32), sds((1, F_IN), F32), sds((1, F_OUT), F32), sds((1, 24), F32)),
-        in_specs=[smem] + [hbm] * 4 + [vmem] * 6,
-        out_specs=(hbm, hbm) + (vmem,) * 6,
+        out_shape=(pltpu.VMEM((2 * HALF, D), F32),) + tuple(pltpu.VMEM(*a) for a in small),
+        in_specs=[smem] * 3 + [hbm] * 10,
+        out_specs=(vmem,) * 7,
         scratch_shapes=[
-            pltpu.VMEM((HALF, D), F32), pltpu.VMEM((HALF, D), F32), pltpu.VMEM((HALF, D), F32), pltpu.VMEM((HALF, D), F32),
+            pltpu.VMEM((24, F_IN), BF16), pltpu.VMEM((24, F_OUT), BF16), pltpu.VMEM((1, 24), F32), pltpu.VMEM((1, F_IN), F32), pltpu.VMEM((1, F_OUT), F32), pltpu.VMEM((1, 24), F32),
+            pltpu.VMEM((HALF, D), F32), pltpu.VMEM((HALF, D), F32), pltpu.VMEM((HALF, D), F32),
             pltpu.VMEM((4, 4, 2, 24, HALF), F32), pltpu.VMEM((4, 4, 2, 24, HALF), F32),
             pltpu.VMEM((2, 4, 24, HALF), F32), pltpu.VMEM((2, 4, 24, HALF), F32), pltpu.VMEM((2, 4, 24, HALF), F32), pltpu.VMEM((2, 4, 24, HALF), F32),
             pltpu.VMEM((2, 24, HALF), F32), pltpu.VMEM((2, 24, HALF), F32), pltpu.VMEM((2, 24, HALF), F32),
@@ -390,16 +398,24 @@
             pltpu.VMEM((1, HALF), F32), pltpu.VMEM((1, HALF), F32), pltpu.VMEM((1, HALF), F32),
             pltpu.VMEM((16, 1, HALF), F32), pltpu.VMEM((4, 2, 8, 128), F32), pltpu.VMEM((4, 2, 8, 128), F32), pltpu.VMEM((16, 8, 128), F32),
             pltpu.VMEM((48, HALF), F32), pltpu.VMEM((24, 128), F32), pltpu.VMEM((24, 256), F32), pltpu.VMEM((1, 128), F32), pltpu.VMEM((1, 256), F32), pltpu.VMEM((8, 128), F32),
-            pltpu.SemaphoreType.DMA((9,)), pltpu.SemaphoreType.DMA((N_SEMS,)), pltpu.SemaphoreType.DMA((N_SEMS,)),
+            pltpu.SemaphoreType.DMA((12,)), pltpu.SemaphoreType.DMA((N_SEMS,)), pltpu.SemaphoreType.DMA((N_SEMS,)),
         ],
-        compiler_params=pltpu.CompilerParams(collective_id=0, has_side_effects=True, vmem_limit_bytes=48 * 1024 * 1024),
+        compiler_params=pltpu.CompilerParams(collective_id=0, has_side_effects=True, vmem_limit_bytes=40 * 1024 * 1024),
     )(*args)
+    return pl.pallas_call(
+        store_kernel,
+        name="store_outputs",
+        out_shape=(sds((F_IN, D), F32), sds((F_OUT, D), F32)) + tuple(sds(*a) for a in small),
+        in_specs=[vmem] * 7,
+        out_specs=(hbm,) * 8,
+        scratch_shapes=[pltpu.SemaphoreType.DMA((9,))],
+        compiler_params=pltpu.CompilerParams(vmem_limit_bytes=16 * 1024 * 1024),
+    )(*held)
 
 
 def solution(mesh):
     def body(w_in, w_out, g_in, g_out, m_in, m_out, r_in, c_in, r_out, c_out, learn_rate, weight_decay, beta_two):
-        scal = jnp.stack([learn_rate, weight_decay, beta_two])
-        outs = call(scal, g_in[0, 0].T, g_out[0, 0], w_in[0].T, w_out[0], m_in[0], m_out[0].T, r_in, c_in, r_out, c_out)
+        outs = call(learn_rate[None], weight_decay[None], beta_two[None], g_in[0, 0].T, g_out[0, 0], w_in[0].T, w_out[0], m_in[0], m_out[0].T, r_in, c_in, r_out, c_out)
         return (outs[0].T[None], outs[1][None], outs[2][None], outs[3].T[None], outs[4], outs[5], outs[6], outs[7])
 
     in_specs = (P(None, None, 'tp'), P(None, 'tp', None), P('dp', None, None, 'tp'), P('dp', None, 'tp', None), P(None, 'dp', 'tp'), P(None, 'tp', 'dp'), P(None, 'dp'), P(None, 'tp'), P(None, 'tp'), P(None, 'dp'), P(), P(), P())

time: 103 us -> 89.4 us (0.87)
  local copies, waits for them, and re-layouts: 15.7 us -> 0 us
  Pallas kernels: 83.9 us -> 86.7 us
    unnamed x22 -> x0, local copies, waits for them, and re-layouts: 15.7 us -> none
    pallas_call x1 -> x2, Pallas kernels: 83.9 us -> 86.7 us  [the longest x1 83.6 us: call(): pl.pallas_call(kernel, name='adafactor_step', out_shape=(pltpu.VMEM((2 *...]
where the time goes in v2:
time: 89.4 us; the launch traced here: 89.2 us
  Pallas kernels  86.7 us (97%)
  between operations  2.58 us (3%)
    pallas_call x1, Pallas kernels, call(): pl.pallas_call(kernel, name='adafactor_step', out_shape=(pltpu.VMEM((2 *...  83.6 us
    pallas_call x1, Pallas kernels, call(): pl.pallas_call(store_kernel, name='store_outputs', out_shape=(sds((F_IN,...  3.04 us

profile of v2, /device:TPU:1, one launch (start us, length us, event | category | flops | bytes accessed | tf_op | source)
XLA Modules:
  0.0 89.2 jit_solution(6810501992250984156)
XLA Ops:
  2.6 83.6 %adafactor_step.1 = (f32[2304,768]{1,0:T(8,128)S(1)}, bf16[24,1344]{1,0:T(8,128)(2,1)S(1)}, bf16[24,960]{1,0:T(8,128)(2,1)S(1)}, f32[1,24]{1,0:T(1,128)S(1)}, f3...) custom-call(f32[1]{0:T(128)} %bitcast.23.lr_ref, f32[1]{0:T(128)} %bitcast.24.wd_ref, ...), custom_call_target="tpu_custom_call" | custom-call | tf_op jit(solution)/shard_map/adafactor_step/pallas_call | solution.py:385
  86.2 3.0 %store_outputs.1 = (f32[1344,768]{1,0:T(8,128)}, f32[960,768]{1,0:T(8,128)}, bf16[24,1344]{1,0:T(8,128)(2,1)}, bf16[24,960]{1,0:T(8,128)(2,1)}, f32[1,24]{1,0:T(...) custom-call(f32[2304,768]{1,0:T(8,128)S(1)} %get-tuple-element.23.w, ...), custom_call_target="tpu_custom_call" | custom-call | tf_op jit(solution)/shard_map/store_outputs/pallas_call | solution.py:405

commit v3 on v0

v3 whole, which is shorter than its diff:
```python
import jax
import jax.numpy as jnp
from jax import lax
from jax.experimental import pallas as pl
from jax.experimental.pallas import tpu as pltpu
from jax.sharding import PartitionSpec as P

MESH = pl.DeviceIdType.MESH
F32 = jnp.float32
BF16 = jnp.bfloat16
ALL = slice(None)

D = 768
F_IN = 1344
F_OUT = 960
HALF = 1152
TAIL = 192
N_IN = 5376
N_OUT = 3840
T = 128
W = 24
RING = 4
REDUCE_SEGS = ((0, 2, 1), (2, 3, 2), (5, 2, 1), (7, 2, 1))
GATHER_SEGS = ((0, 3, 2), (3, 2, 1), (5, 2, 1), (7, 2, 1))
ROWS_ONE = pl.ds(0, 1)
N_SEND = 13
N_RECV = 44
N_LOAD = 11


def spans(half, lo, hi):
    if half == 0:
        return [(0, lo, lo, hi - lo)]
    out = []
    if lo < F_OUT:
        out.append((1, lo, lo, min(hi, F_OUT) - lo))
    if hi > F_OUT:
        start = max(lo, F_OUT)
        out.append((0, start + TAIL, start, hi - start))
    return out


def join_tail(out_val, tail_val, pad_a, pad_b):
    pad_a[...] = jnp.zeros_like(pad_a)
    pad_b[...] = jnp.zeros_like(pad_b)
    cut = F_OUT - F_OUT % T
    pad_a[:, :F_OUT - cut] = out_val[:, cut:]
    pad_b[:, :TAIL] = tail_val
    moved = pltpu.roll(pad_b[...], F_OUT - cut, 1)
    lane = lax.broadcasted_iota(jnp.int32, pad_a.shape, 1)
    mid = jnp.where(lane < F_OUT - cut, pad_a[...], moved[:, :T])
    return jnp.concatenate([out_val[:, :cut], mid, moved[:, T:]], axis=1)


def kernel(lr_ref, wd_ref, beta_ref, g_in, g_out, w_in, w_out, h_m_in, h_m_out, h_r_in, h_c_in, h_r_out, h_c_out,
           o_w, o_m_in, o_m_out, o_r_in, o_c_in, o_r_out, o_c_out,
           m_in, m_out, r_in, c_in, r_out, c_out,
           xown, xrecv, wown, tbuf, t2buf, far, dc, pbuf, far2, dc2,
           mx, ms, mrecv, fo, fnew, frecv, fv, rv, qa, qb, gb, pad_a, pad_b, pad_c, pad_d, rowpad,
           load_sem, send, recv):
    x = lax.axis_index("tp")
    d = lax.axis_index("dp")
    core = lax.rem(d, 2)
    p = lax.div(d, 2)
    y = lax.rem(p, RING)
    z = lax.div(p, RING)
    on_first = core == 0
    line_me = x * 2 + core

    def at(xx, pp, cc):
        return (xx, pp * 2 + cc)

    def step(i, k):
        return lax.rem(i + k, RING)

    partner = at(x, p, 1 - core)
    sends = iter(range(N_SEND))
    recvs = iter(range(N_RECV))
    loads = iter(range(N_LOAD))

    def remote(src, dst, dev, s, r):
        c = pltpu.make_async_remote_copy(src_ref=src, dst_ref=dst, send_sem=send.at[s], recv_sem=recv.at[r], device_id=dev, device_id_type=MESH)
        c.start()

    def wait(ref, sem):
        pltpu.make_async_copy(ref, ref, sem).wait()

    x_load = [next(loads) for _ in REDUCE_SEGS]
    w_load = next(loads)
    for me in range(2):
        @pl.when(core == me)
        def _():
            for (t0, n, _), sem in zip(REDUCE_SEGS, x_load):
                for which, lo, to, rows in spans(me, t0 * T, (t0 + n) * T):
                    pltpu.make_async_copy((g_in, g_out)[which].at[pl.ds(lo, rows)], xown.at[pl.ds(to, rows)], load_sem.at[sem]).start()
            for which, lo, to, rows in spans(me, 0, HALF):
                pltpu.make_async_copy((w_in, w_out)[which].at[pl.ds(lo, rows)], wown.at[pl.ds(to, rows)], load_sem.at[w_load]).start()
    small = [pltpu.make_async_copy(src, dst, load_sem.at[next(loads)]) for src, dst in (
        (h_m_in, m_in), (h_m_out, m_out), (h_r_in, r_in), (h_c_in, c_in), (h_r_out, r_out), (h_c_out, c_out))]
    for c in small:
        c.start()

    barrier = pltpu.get_barrier_semaphore()
    ring = ((y, at(x, z * RING + step(y, 1), core), at(x, z * RING + step(y, 3), core)),
            (z, at(x, step(z, 1) * RING + y, core), at(x, step(z, 3) * RING + y, core)))
    line = []
    for k in range(1, 8):
        other = lax.rem(line_me + k, 8)
        line.append(at(lax.div(other, 2), p, lax.rem(other, 2)))
    plane = [at(x, lax.rem(p + k, 16), core) for k in range(1, 16)]
    greet = [dev for _, right, left in ring for dev in (right, left)] + line
    for dev in greet:
        pl.semaphore_signal(barrier, inc=1, device_id=dev, device_id_type=MESH)
    pl.semaphore_wait(barrier, len(greet))

    swap_send = next(sends)
    swap_recv = [next(recvs) for _ in REDUCE_SEGS]
    for me in range(2):
        @pl.when(core == me)
        def _():
            for (t0, n, _), sem in zip(REDUCE_SEGS, swap_recv):
                for which, lo, to, rows in spans(1 - me, t0 * T, (t0 + n) * T):
                    remote((g_in, g_out)[which].at[pl.ds(lo, rows)], xrecv.at[pl.ds(to, rows)], partner, swap_send, sem)

    def lanes_of(seg):
        t0, n, n_a = seg
        return pl.ds(t0 * T, n_a * T), pl.ds((t0 + n_a) * T, (n - n_a) * T), pl.ds(t0 * T, n * T)

    blocks = [(i // 8, i // 2 % RING, i % 2) for i in range(16)]

    def transpose_in(j, _):
        rows = pl.ds(pl.multiple_of(j * T, T), T)
        for h in range(2):
            cols = pl.ds(h * D // 2, D // 2)
            t = (xown[rows, cols] + xrecv[rows, cols]).T
            for i, (zz, yy, a) in enumerate(blocks):
                tbuf[2 * h + zz, yy, a, :, rows] = t[W * i:W * i + W]
        return 0

    def chunk(buf, a, k, lanes):
        return buf.at[:, k, 0, :, lanes] if a == 0 else buf.at[k, :, 1, :, lanes]

    send_1, send_2 = next(sends), next(sends)
    far_sem, dc_sem, far2_sem, dc2_sem = ([next(recvs) for _ in REDUCE_SEGS] for _ in range(4))

    def rs_ring(a, phase):
        i, right, left = ring[a if phase == 1 else 1 - a]
        return i, right, left, step(i, 1), step(i, 3), step(i, 2)

    def rs_refs(phase):
        if phase == 1:
            return (lambda a, k, lanes: chunk(tbuf, a, k, lanes), lambda a, lanes: far.at[a, :, :, lanes],
                    lambda kind, a, lanes: dc.at[kind, a, :, :, lanes], send_1, far_sem, dc_sem)
        return (lambda a, k, lanes: pbuf.at[a, k, :, lanes], lambda a, lanes: far2.at[a, :, lanes],
                lambda kind, a, lanes: dc2.at[kind, a, :, lanes], send_2, far2_sem, dc2_sem)

    def rs_begin(s, phase):
        la, lb, _ = lanes_of(REDUCE_SEGS[s])
        src, far_at, dc_at, ss, fs, ds = rs_refs(phase)
        for a in range(2):
            i, right, left, r, l, f = rs_ring(a, phase)
            remote(src(a, f, la), far_at(a, la), right, ss, fs[s])
            remote(src(a, f, lb), far_at(a, lb), left, ss, fs[s])
        for a in range(2):
            i, right, left, r, l, f = rs_ring(a, phase)
            remote(src(a, r, lb), dc_at(0, a, lb), right, ss, ds[s])
            remote(src(a, l, la), dc_at(0, a, la), left, ss, ds[s])

    def rs_middle(s, phase):
        la, lb, full = lanes_of(REDUCE_SEGS[s])
        src, far_at, dc_at, ss, fs, ds = rs_refs(phase)
        wait((far.at[:, :, :, full] if phase == 1 else far2.at[:, :, full]), recv.at[fs[s]])
        for a in range(2):
            i, right, left, r, l, f = rs_ring(a, phase)
            for k, lanes, dev in ((r, la, right), (l, lb, left)):
                if phase == 1:
                    for q in range(RING):
                        where = (q, k, 0) if a == 0 else (k, q, 1)
                        tbuf[(*where, ALL, lanes)] += far[a, q, :, lanes]
                else:
                    pbuf[a, k, :, lanes] += far2[a, :, lanes]
                remote(src(a, k, lanes), dc_at(1, a, lanes), dev, ss, ds[s])

    def rs_end(s, phase):
        _, _, full = lanes_of(REDUCE_SEGS[s])
        wait((dc.at[:, :, :, :, full] if phase == 1 else dc2.at[:, :, :, full]), recv.at[rs_refs(phase)[-1][s]])
        for a in range(2):
            i = rs_ring(a, phase)[0]
            if phase == 1:
                for q in range(RING):
                    where = (q, i, 0) if a == 0 else (i, q, 1)
                    pbuf[a, q, :, full] = tbuf[(*where, ALL, full)] + dc[0, a, q, :, full] + dc[1, a, q, :, full]
            else:
                gb[W * a:W * a + W, full] = pbuf[a, i, :, full] + dc2[0, a, :, full] + dc2[1, a, :, full]

    def prepare():
        for c in small:
            c.wait()
        first = m_in[:, :HALF].astype(F32)
        second = join_tail(m_out[...].astype(F32), m_in[:, HALF:].astype(F32), pad_a, pad_b)
        mx[core] = jnp.where(on_first, first, second)
        ms[...] = jnp.where(on_first, second, first)
        remote(ms, mx.at[core], partner, m_send, m_recv)
        fo[...] = jnp.where(on_first, c_in[:, :HALF], join_tail(r_out[...], c_in[:, HALF:], pad_c, pad_d))

    m_send, m_recv = next(sends), next(recvs)
    n_segs = len(REDUCE_SEGS)
    for t in range(n_segs + RING):
        if t < n_segs:
            t0, n, _ = REDUCE_SEGS[t]
            rows = pl.ds(t0 * T, n * T)
            wait(xown.at[rows], load_sem.at[x_load[t]])
            wait(xown.at[rows], recv.at[swap_recv[t]])
            lax.fori_loop(t0, t0 + n, transpose_in, 0)
            rs_begin(t, 1)
        if t == 1:
            prepare()
        for lag, work in enumerate((lambda s: rs_middle(s, 1), lambda s: (rs_end(s, 1), rs_begin(s, 2)), lambda s: rs_middle(s, 2), lambda s: rs_end(s, 2))):
            s = t - 1 - lag
            if 0 <= s < n_segs:
                work(s)

    lane = lax.broadcasted_iota(jnp.int32, (1, HALF), 1)
    is_in = lane >= jnp.where(on_first, 0, F_OUT)
    eye = lax.broadcasted_iota(jnp.int32, (2 * W, T), 0) == lax.broadcasted_iota(jnp.int32, (2 * W, T), 1)

    def sum_of(v, axis):
        return jnp.sum(v, axis=axis, keepdims=True)

    def only_in(v):
        return jnp.where(is_in, v, 0.0)

    def only_out(v):
        return jnp.where(is_in, 0.0, v)

    def to_row(col):
        return sum_of(jnp.where(eye, col, 0.0), 0)

    def to_col(row):
        return sum_of(jnp.where(eye, row, 0.0), 1)

    def spread(slots, me, devs):
        ss, rs = next(sends), next(recvs)
        for dev in devs:
            remote(slots.at[me], slots.at[me], dev, ss, rs)
        return slots.at[pl.ds(0, len(devs))], ss, rs

    g = gb[...]
    sq = g * g + 1e-30
    fv[p] = sum_of(sq, 0)
    fv_ref, fv_send, fv_recv = spread(fv, p, plane)
    for row, col in enumerate((only_in(sq), only_out(sq))):
        rv[line_me, row:row + 1, :] = to_row(sum_of(col, 1))
    for row, ref in ((2, r_in), (3, c_out)):
        rowpad[...] = jnp.zeros_like(rowpad)
        rowpad[ROWS_ONE, :W] = ref[...]
        rv[line_me, row:row + 1, :] = jnp.where(on_first, rowpad[...], pltpu.roll(rowpad[...], W, 1))[:1]
    rv[line_me, RING:, :] = jnp.zeros((RING, T), F32)
    rv_ref, rv_send, rv_recv = spread(rv, line_me, line)

    lr, wd, beta = lr_ref[0], wd_ref[0], beta_ref[0]
    wait(rv_ref, recv.at[rv_recv])
    row_sum = jnp.sum(rv[...], axis=0)
    row_old = rv[0] + rv[1]
    r_new = beta * row_old[2:3] + (1.0 - beta) * (row_sum[:1] / N_IN)
    c_new = beta * row_old[3:4] + (1.0 - beta) * (row_sum[1:2] / N_OUT)
    v = g * jnp.where(is_in, 1.0 / jnp.sqrt(to_col(r_new)), 1.0 / jnp.sqrt(to_col(c_new)))
    sum_rows = sum_of(r_new, 1)
    wait(fv_ref, recv.at[fv_recv])
    f_new = beta * fo[...] + (1.0 - beta) * (jnp.sum(fv[...], axis=0) / D)
    u = v * (1.0 / jnp.sqrt(f_new))
    uu = u * u
    f_out = sum_of(only_out(f_new), 1)

    def total(v):
        return jnp.broadcast_to(sum_of(sum_of(v, 0), 1), (1, T))

    qa[line_me] = jnp.concatenate([total(only_in(uu)), total(only_out(uu)), jnp.broadcast_to(f_out, (6, T))], axis=0)
    qa_ref, qa_send, qa_recv = spread(qa, line_me, line)
    gb[...] = u
    fnew[...] = f_new
    f_send, f_recv = next(sends), next(recvs)
    remote(fnew, frecv, partner, f_send, f_recv)
    wait(qa_ref, recv.at[qa_recv])
    line_sum = jnp.sum(qa[...], axis=0)
    qb[p] = jnp.concatenate([line_sum[:2], jnp.broadcast_to(sum_rows, (6, T))], axis=0)
    qb_ref, qb_send, qb_recv = spread(qb, p, plane)
    wait(mx.at[0], recv.at[m_recv])
    wait(qb_ref, recv.at[qb_recv])
    plane_sum = jnp.sum(qb[...], axis=0)[:, :1]
    mean_in = plane_sum[2:3] / D
    mean_out = line_sum[2:3, :1] / N_OUT
    rms_in = jnp.sqrt(plane_sum[:1] * mean_in / (D * N_IN))
    rms_out = jnp.sqrt(plane_sum[1:2] * mean_out / (D * N_OUT))
    scale = jnp.where(is_in, jnp.sqrt(mean_in) / jnp.maximum(1.0, rms_in), jnp.sqrt(mean_out) / jnp.maximum(1.0, rms_out))

    for a in range(2):
        t2buf[z, y, a] = (0.9 * mx[a] + 0.1 * (gb[W * a:W * a + W] * scale)).astype(BF16).astype(F32)

    send_3, send_4 = next(sends), next(sends)
    first_sem, rest_sem, first2_sem, rest2_sem = ([next(recvs) for _ in GATHER_SEGS] for _ in range(4))

    def ag_refs(phase):
        if phase == 1:
            return (lambda a, k, lanes: t2buf.at[k, y, 0, :, lanes] if a == 0 else t2buf.at[z, k, 1, :, lanes]), send_3, first_sem, rest_sem
        return (lambda a, k, lanes: chunk(t2buf, a, k, lanes)), send_4, first2_sem, rest2_sem

    def ag_begin(s, phase):
        la, lb, _ = lanes_of(GATHER_SEGS[s])
        ref, ss, fs, rs = ag_refs(phase)
        for lanes_r, lanes_l, sem in ((la, lb, fs[s]), (lb, la, rs[s])):
            for a in range(2):
                i, right, left, r, l, f = rs_ring(a, 3 - phase)
                remote(ref(a, i, lanes_r), ref(a, i, lanes_r), right, ss, sem)
                remote(ref(a, i, lanes_l), ref(a, i, lanes_l), left, ss, sem)

    def ag_middle(s, phase):
        la, lb, full = lanes_of(GATHER_SEGS[s])
        ref, ss, fs, rs = ag_refs(phase)
        wait((far2.at[:, :, full] if phase == 1 else far.at[:, :, :, full]), recv.at[fs[s]])
        for a in range(2):
            i, right, left, r, l, f = rs_ring(a, 3 - phase)
            remote(ref(a, l, la), ref(a, l, la), right, ss, rs[s])
            remote(ref(a, r, lb), ref(a, r, lb), left, ss, rs[s])

    def ag_end(s, phase):
        full = lanes_of(GATHER_SEGS[s])[-1]
        wait((dc2.at[:, :, :, full] if phase == 1 else dc.at[:, :, :, :, full]), recv.at[ag_refs(phase)[-1][s]])

    lr_wd = lr * wd
    base = core * HALF

    def transpose_out(j, _):
        rows = pl.ds(pl.multiple_of(j * T, T), T)
        dest = pl.ds(pl.multiple_of(base + j * T, T), T)
        for h in range(2):
            cols = pl.ds(h * D // 2, D // 2)
            t = jnp.concatenate([t2buf[2 * h + zz, yy, a, :, rows] for zz, yy, a in blocks], axis=0)
            w = wown[rows, cols]
            o_w[dest, cols] = w - lr * t.T - lr_wd * w
        return 0

    mo_send, mo_recv = next(sends), next(recvs)
    out_send, out_recv = next(sends), next(recvs)

    def state_out():
        remote(t2buf.at[z, y, 1 - core], mrecv, partner, mo_send, mo_recv)
        wait(frecv, recv.at[f_recv])
        wait(mrecv, recv.at[mo_recv])
        for mine, theirs, out_in, out_out in ((t2buf[z, y, core], mrecv[...], o_m_in, o_m_out), (fnew[...], frecv[...], o_c_in, o_r_out)):
            lo = jnp.where(on_first, mine, theirs)
            hi = jnp.where(on_first, theirs, mine)
            out_in[:, :HALF] = lo.astype(out_in.dtype)
            out_out[...] = hi[:, :F_OUT].astype(out_out.dtype)
            out_in[:, HALF:] = pltpu.roll(hi[:, HALF - 2 * T:], TAIL, 1)[:, :TAIL].astype(out_in.dtype)
        for new, out in ((r_new, o_r_in), (c_new, o_c_out)):
            rowpad[...] = jnp.broadcast_to(new, rowpad.shape)
            out[...] = jnp.where(on_first, rowpad[...], pltpu.roll(rowpad[...], T - W, 1))[:1, :W]
        wait(wown, load_sem.at[w_load])

    def finish(s):
        ag_end(s, 2)
        t0, n, _ = GATHER_SEGS[s]
        lax.fori_loop(t0, t0 + n, transpose_out, 0)
        span = pl.ds(pl.multiple_of(base + t0 * T, T), n * T)
        remote(o_w.at[span], o_w.at[span], partner, out_send, out_recv)

    n_segs = len(GATHER_SEGS)
    for t in range(n_segs + RING):
        if t < n_segs:
            ag_begin(t, 1)
        if t == 3:
            state_out()
        for lag, work in enumerate((lambda s: ag_middle(s, 1), lambda s: (ag_end(s, 1), ag_begin(s, 2)), lambda s: ag_middle(s, 2), finish)):
            s = t - 1 - lag
            if 0 <= s < n_segs:
                work(s)

    wait(xown, recv.at[out_recv])
    for ref, sem in ((xown, swap_send), (ms, m_send), (tbuf.at[:3], send_1), (tbuf.at[0, :3], send_2), (fv_ref, fv_send), (rv_ref, rv_send), (qa_ref, qa_send), (qb_ref, qb_send),
                     (fnew, f_send), (t2buf.at[0, :3], send_3), (t2buf.at[:3], send_4), (ms, mo_send), (xown, out_send)):
        wait(ref, send.at[sem])


def store_kernel(w, m_in, m_out, r_in, c_in, r_out, c_out, o_w_in, o_w_out, o_m_in, o_m_out, o_r_in, o_c_in, o_r_out, o_c_out, sem):
    pairs = [(w.at[pl.ds(0, HALF)], o_w_in.at[pl.ds(0, HALF)]), (w.at[pl.ds(HALF, F_OUT)], o_w_out), (w.at[pl.ds(HALF + F_OUT, TAIL)], o_w_in.at[pl.ds(HALF, TAIL)]),
             (m_in, o_m_in), (m_out, o_m_out), (r_in, o_r_in), (c_in, o_c_in), (r_out, o_r_out), (c_out, o_c_out)]
    work = [pltpu.make_async_copy(src, dst, sem.at[n]) for n, (src, dst) in enumerate(pairs)]
    for c in work:
        c.start()
    for c in work:
        c.wait()


def call(*args):
    vmem = pl.BlockSpec(memory_space=pltpu.VMEM)
    hbm = pl.BlockSpec(memory_space=pltpu.HBM)
    smem = pl.BlockSpec(memory_space=pltpu.SMEM)
    small = (((W, F_IN), BF16), ((W, F_OUT), BF16), ((1, W), F32), ((1, F_IN), F32), ((1, F_OUT), F32), ((1, W), F32))
    in_vmem = [pltpu.VMEM(*a) for a in small]
    args = args[:3] + tuple(pltpu.with_memory_space_constraint(a, pltpu.HBM) for a in args[3:])

    def buf(*shape):
        return pltpu.VMEM(shape, F32)

    half, whole, part, line = (HALF, D), (RING, RING, 2, W, HALF), (W, HALF), (1, HALF)
    held = pl.pallas_call(
        kernel,
        name="adafactor_step",
        out_shape=(buf(2 * HALF, D), *in_vmem),
        in_specs=[smem] * 3 + [hbm] * (len(args) - 3),
        out_specs=(vmem,) * (1 + len(small)),
        scratch_shapes=[
            *in_vmem, buf(*half), buf(*half), buf(*half), buf(*whole), buf(*whole),
            buf(2, RING, *part), buf(2, 2, RING, *part), buf(2, RING, *part), buf(2, *part), buf(2, 2, *part),
            buf(2, *part), buf(*part), buf(*part), buf(*line), buf(*line), buf(*line),
            buf(16, *line), buf(8, 8, T), buf(8, 8, T), buf(16, 8, T),
            buf(2 * W, HALF), buf(W, T), buf(W, 2 * T), buf(1, T), buf(1, 2 * T), buf(8, T),
            pltpu.SemaphoreType.DMA((N_LOAD,)), pltpu.SemaphoreType.DMA((N_SEND,)), pltpu.SemaphoreType.DMA((N_RECV,)),
        ],
        compiler_params=pltpu.CompilerParams(collective_id=0, has_side_effects=True, vmem_limit_bytes=40 << 20),
    )(*args)
    return pl.pallas_call(
        store_kernel,
        name="store_outputs",
        out_shape=tuple(jax.ShapeDtypeStruct(*a) for a in (((F_IN, D), F32), ((F_OUT, D), F32), *small)),
        in_specs=[vmem] * (1 + len(small)),
        out_specs=(hbm,) * (2 + len(small)),
        scratch_shapes=[pltpu.SemaphoreType.DMA((9,))],
        compiler_params=pltpu.CompilerParams(vmem_limit_bytes=16 << 20),
    )(*held)


def solution(mesh):
    def body(w_in, w_out, g_in, g_out, m_in, m_out, r_in, c_in, r_out, c_out, learn_rate, weight_decay, beta_two):
        outs = call(learn_rate[None], weight_decay[None], beta_two[None], g_in[0, 0].T, g_out[0, 0], w_in[0].T, w_out[0], m_in[0], m_out[0].T, r_in, c_in, r_out, c_out)
        return (outs[0].T[None], outs[1][None], outs[2][None], outs[3].T[None], *outs[4:])

    rows, cols, f_last, f_mid = P(None, 'dp'), P(None, 'tp'), P(None, None, 'tp'), P(None, 'tp', None)
    m_specs = (P(None, 'dp', 'tp'), P(None, 'tp', 'dp'))
    stats = (rows, cols, cols, rows)
    in_specs = (f_last, f_mid, P('dp', None, None, 'tp'), P('dp', None, 'tp', None), *m_specs, *stats, P(), P(), P())
    return jax.shard_map(body, mesh=mesh, in_specs=in_specs, out_specs=(f_last, f_mid, *m_specs, *stats), check_vma=False)
```

time: 498 us -> 83.7 us (0.17)
  waiting for transfers between devices: 239 us -> 0 us
  blocking collectives: 206 us -> 0 us
  Pallas kernels: 0 us -> 81 us
  local copies, waits for them, and re-layouts: 22.6 us -> 0 us
  between operations: 18.5 us -> 2.58 us
  other arithmetic: 11.2 us -> 0 us
    psum x4 -> x0, blocking collectives: 206 us -> none  [the longest x2 129 us: local_update(): row_avg = lax.psum(jnp.sum(row_new, axis=1), row_axis) / n_rows]
    all_gather x2 -> x0, waiting for transfers between devices: 81.8 us -> none  [local_update(): w_new = lax.all_gather(w_block, 'dp', axis=dp_dim, tiled=True)]
    unnamed x5 -> x0, waiting for transfers between devices: 81.4 us -> none
    pallas_call x0 -> x2, Pallas kernels: none -> 81 us  [the longest x1 77.9 us: call(): pl.pallas_call(kernel, name='adafactor_step', out_shape=(buf(2 * HALF, D)...]
    reduce_scatter x1 -> x0, waiting for transfers between devices: 75.3 us -> none  [local_update(): lax.psum_scatter(grad_rep[0], 'dp', scatter_dimension=dp_dim, tiled=True)]
    unnamed x20 -> x0, local copies, waits for them, and re-layouts: 20 us -> none
    reduce_sum x6 -> x0, other arithmetic: 7.17 us -> none  [the longest x2 3.23 us: local_update(): total_sq = lax.psum(jnp.sum(update * update, axis=(1, 2)), ('tp', 'dp'))]
  transfers between devices with their start and end apart: 4 -> 0, of which waited for: 4 -> 0; matrix products, arithmetic and copies ran while one was open for 3% -> 0% of each run, Pallas kernels for 0% -> 0%
where the time goes in v3:
time: 83.7 us; the launch traced here: 83.6 us
  Pallas kernels  81 us (97%)
  between operations  2.58 us (3%)
    pallas_call x1, Pallas kernels, call(): pl.pallas_call(kernel, name='adafactor_step', out_shape=(buf(2 * HALF, D)...  77.9 us
    pallas_call x1, Pallas kernels, call(): pl.pallas_call(store_kernel, name='store_outputs', out_shape=tuple((jax.S...  3.04 us

profile of v3, /device:TPU:1, one launch (start us, length us, event | category | flops | bytes accessed | tf_op | source)
XLA Modules:
  0.0 83.6 jit_solution(11853013593636485428)
XLA Ops:
  2.6 77.9 %adafactor_step.1 = (f32[2304,768]{1,0:T(8,128)S(1)}, bf16[24,1344]{1,0:T(8,128)(2,1)S(1)}, bf16[24,960]{1,0:T(8,128)(2,1)S(1)}, f32[1,24]{1,0:T(1,128)S(1)}, f3...) custom-call(f32[1]{0:T(128)} %bitcast.23.lr_ref, f32[1]{0:T(128)} %bitcast.24.wd_ref, ...), custom_call_target="tpu_custom_call" | custom-call | tf_op jit(solution)/shard_map/adafactor_step/pallas_call | solution.py:407
  80.5 3.0 %store_outputs.1 = (f32[1344,768]{1,0:T(8,128)}, f32[960,768]{1,0:T(8,128)}, bf16[24,1344]{1,0:T(8,128)(2,1)}, bf16[24,960]{1,0:T(8,128)(2,1)}, f32[1,24]{1,0:T(...) custom-call(f32[2304,768]{1,0:T(8,128)S(1)} %get-tuple-element.23.w, ...), custom_call_target="tpu_custom_call" | custom-call | tf_op jit(solution)/shard_map/store_outputs/pallas_call | solution.py:423

commit v4 on v3

--- a/solution.py
+++ b/solution.py
@@ -20,12 +20,18 @@
 T = 128
 W = 24
 RING = 4
-REDUCE_SEGS = ((0, 2, 1), (2, 3, 2), (5, 2, 1), (7, 2, 1))
-GATHER_SEGS = ((0, 3, 2), (3, 2, 1), (5, 2, 1), (7, 2, 1))
+REDUCE_SEGS = ((0, 2, 1), (2, 2, 1), (4, 5, 2))
+GATHER_SEGS = ((0, 3, 2), (3, 4, 2), (7, 2, 1))
+REDUCE_UNITS = ((None,), (None,), (2, 1, 3, 0))
+BLOCKS = (0, 1, 3, 2)
+GATHER_UNITS = (((0,), (1, 3), (2,)), ((0,), (1, 3), (2,)), (None,))
+RELAY_LAST = (True, False, False)
+REDUCE_PLAN = ("S0,B00,S1,B10,M00,S2,B20,B21,B22,B23,H0,M10,E00", "M20,M21,M22,M23,E10,C0,E20,E21,E22,E23,F1,F0,F2")
+GATHER_PLAN = ("A0,B00,A1,A2,M0,N0,B01,P00,M1,N1,M2,N2,W0,B02,B10,B11", "P01,W1,W2,B12,P02,P10,B20,P11,P12,F0,P20,F1,F2")
 ROWS_ONE = pl.ds(0, 1)
-N_SEND = 13
-N_RECV = 44
-N_LOAD = 11
+N_SEND = 11
+N_RECV = 45
+N_LOAD = 10
 
 
 def spans(half, lo, hi):
@@ -56,7 +62,7 @@
            o_w, o_m_in, o_m_out, o_r_in, o_c_in, o_r_out, o_c_out,
            m_in, m_out, r_in, c_in, r_out, c_out,
            xown, xrecv, wown, tbuf, t2buf, far, dc, pbuf, far2, dc2,
-           mx, ms, mrecv, fo, fnew, frecv, fv, rv, qa, qb, gb, pad_a, pad_b, pad_c, pad_d, rowpad,
+           mx, ms, mrecv, fo, fnew, frecv, fv, rv, qs, gb, pad_a, pad_b, pad_c, pad_d, rowpad,
            load_sem, send, recv):
     x = lax.axis_index("tp")
     d = lax.axis_index("dp")
@@ -101,14 +107,14 @@
         c.start()
 
     barrier = pltpu.get_barrier_semaphore()
-    ring = ((y, at(x, z * RING + step(y, 1), core), at(x, z * RING + step(y, 3), core)),
-            (z, at(x, step(z, 1) * RING + y, core), at(x, step(z, 3) * RING + y, core)))
+    ring = ((y, *(at(x, z * RING + step(y, k), core) for k in (1, 3, 2))),
+            (z, *(at(x, step(z, k) * RING + y, core) for k in (1, 3, 2))))
     line = []
     for k in range(1, 8):
         other = lax.rem(line_me + k, 8)
         line.append(at(lax.div(other, 2), p, lax.rem(other, 2)))
     plane = [at(x, lax.rem(p + k, 16), core) for k in range(1, 16)]
-    greet = [dev for _, right, left in ring for dev in (right, left)] + line
+    greet = [dev for _, right, left, _ in ring for dev in (right, left)] + line
     for dev in greet:
         pl.semaphore_signal(barrier, inc=1, device_id=dev, device_id_type=MESH)
     pl.semaphore_wait(barrier, len(greet))
@@ -137,63 +143,100 @@
                 tbuf[2 * h + zz, yy, a, :, rows] = t[W * i:W * i + W]
         return 0
 
-    def chunk(buf, a, k, lanes):
-        return buf.at[:, k, 0, :, lanes] if a == 0 else buf.at[k, :, 1, :, lanes]
+    cross = (z, y)
+
+    def spot(a, k, q):
+        return (q, k, 0) if a == 0 else (k, q, 1)
+
+    def piece(buf, a, k, q, lanes):
+        return buf.at[(*spot(a, k, q), ALL, lanes)]
+
+    def ring_of(a):
+        i, right, left, _ = ring[a]
+        return i, right, left, step(i, 1), step(i, 3), step(i, 2)
+
+    def block(a, off):
+        return ALL if off is None else step(cross[a], off)
 
     send_1, send_2 = next(sends), next(sends)
-    far_sem, dc_sem, far2_sem, dc2_sem = ([next(recvs) for _ in REDUCE_SEGS] for _ in range(4))
-
-    def rs_ring(a, phase):
-        i, right, left = ring[a if phase == 1 else 1 - a]
-        return i, right, left, step(i, 1), step(i, 3), step(i, 2)
-
-    def rs_refs(phase):
-        if phase == 1:
-            return (lambda a, k, lanes: chunk(tbuf, a, k, lanes), lambda a, lanes: far.at[a, :, :, lanes],
-                    lambda kind, a, lanes: dc.at[kind, a, :, :, lanes], send_1, far_sem, dc_sem)
-        return (lambda a, k, lanes: pbuf.at[a, k, :, lanes], lambda a, lanes: far2.at[a, :, lanes],
-                lambda kind, a, lanes: dc2.at[kind, a, :, lanes], send_2, far2_sem, dc2_sem)
-
-    def rs_begin(s, phase):
+    far_sem, dc_sem = ([[next(recvs) for _ in u] for u in REDUCE_UNITS] for _ in range(2))
+    dc2_sem = [next(recvs) for _ in REDUCE_SEGS]
+    far2_sem = [next(recvs) if relay else None for relay in RELAY_LAST]
+
+    def rs_begin(s, u):
         la, lb, _ = lanes_of(REDUCE_SEGS[s])
-        src, far_at, dc_at, ss, fs, ds = rs_refs(phase)
-        for a in range(2):
-            i, right, left, r, l, f = rs_ring(a, phase)
-            remote(src(a, f, la), far_at(a, la), right, ss, fs[s])
-            remote(src(a, f, lb), far_at(a, lb), left, ss, fs[s])
-        for a in range(2):
-            i, right, left, r, l, f = rs_ring(a, phase)
-            remote(src(a, r, lb), dc_at(0, a, lb), right, ss, ds[s])
-            remote(src(a, l, la), dc_at(0, a, la), left, ss, ds[s])
-
-    def rs_middle(s, phase):
+        off = REDUCE_UNITS[s][u]
+        for a in range(2):
+            i, right, left, r, l, f = ring_of(a)
+            q = block(a, off)
+            remote(piece(tbuf, a, f, q, la), far.at[a, q, :, la], right, send_1, far_sem[s][u])
+            remote(piece(tbuf, a, f, q, lb), far.at[a, q, :, lb], left, send_1, far_sem[s][u])
+        for a in range(2):
+            i, right, left, r, l, f = ring_of(a)
+            q = block(a, off)
+            remote(piece(tbuf, a, r, q, lb), dc.at[0, a, q, :, lb], right, send_1, dc_sem[s][u])
+            remote(piece(tbuf, a, l, q, la), dc.at[0, a, q, :, la], left, send_1, dc_sem[s][u])
+
+    def unit_blocks(off):
+        return pl.ds(0, RING if off is None else 1)
+
+    def rs_middle(s, u):
         la, lb, full = lanes_of(REDUCE_SEGS[s])
-        src, far_at, dc_at, ss, fs, ds = rs_refs(phase)
-        wait((far.at[:, :, :, full] if phase == 1 else far2.at[:, :, full]), recv.at[fs[s]])
-        for a in range(2):
-            i, right, left, r, l, f = rs_ring(a, phase)
+        off = REDUCE_UNITS[s][u]
+        wait(far.at[:, unit_blocks(off), :, full], recv.at[far_sem[s][u]])
+        for a in range(2):
+            i, right, left, r, l, f = ring_of(a)
+            q = block(a, off)
             for k, lanes, dev in ((r, la, right), (l, lb, left)):
-                if phase == 1:
-                    for q in range(RING):
-                        where = (q, k, 0) if a == 0 else (k, q, 1)
-                        tbuf[(*where, ALL, lanes)] += far[a, q, :, lanes]
-                else:
-                    pbuf[a, k, :, lanes] += far2[a, :, lanes]
-                remote(src(a, k, lanes), dc_at(1, a, lanes), dev, ss, ds[s])
-
-    def rs_end(s, phase):
-        _, _, full = lanes_of(REDUCE_SEGS[s])
-        wait((dc.at[:, :, :, :, full] if phase == 1 else dc2.at[:, :, :, full]), recv.at[rs_refs(phase)[-1][s]])
-        for a in range(2):
-            i = rs_ring(a, phase)[0]
-            if phase == 1:
-                for q in range(RING):
-                    where = (q, i, 0) if a == 0 else (i, q, 1)
-                    pbuf[a, q, :, full] = tbuf[(*where, ALL, full)] + dc[0, a, q, :, full] + dc[1, a, q, :, full]
+                tbuf[(*spot(a, k, q), ALL, lanes)] += far[a, q, :, lanes]
+                remote(piece(tbuf, a, k, q, lanes), dc.at[1, a, q, :, lanes], dev, send_1, dc_sem[s][u])
+
+    def rs_end(s, u):
+        la, lb, full = lanes_of(REDUCE_SEGS[s])
+        off = REDUCE_UNITS[s][u]
+        wait(dc.at[:, :, unit_blocks(off), :, full], recv.at[dc_sem[s][u]])
+        for a in range(2):
+            q = block(a, off)
+            pbuf[a, q, :, full] = tbuf[(*spot(a, ring_of(a)[0], q), ALL, full)] + dc[0, a, q, :, full] + dc[1, a, q, :, full]
+        for a in range(2):
+            i, right, left, r, l, f = ring_of(1 - a)
+            if RELAY_LAST[s]:
+                remote(pbuf.at[a, f, :, la], far2.at[a, :, la], right, send_2, far2_sem[s])
+                remote(pbuf.at[a, f, :, lb], far2.at[a, :, lb], left, send_2, far2_sem[s])
+                remote(pbuf.at[a, r, :, lb], dc2.at[0, a, :, lb], right, send_2, dc2_sem[s])
+                remote(pbuf.at[a, l, :, la], dc2.at[0, a, :, la], left, send_2, dc2_sem[s])
             else:
-                gb[W * a:W * a + W, full] = pbuf[a, i, :, full] + dc2[0, a, :, full] + dc2[1, a, :, full]
-
-    def prepare():
+                for slot, (k, o, dev) in enumerate(((f, 2, ring[1 - a][-1]), (r, 1, right), (l, 3, left))):
+                    if off is None or off == o:
+                        remote(pbuf.at[a, k, :, full], dc2.at[slot, a, :, full], dev, send_2, dc2_sem[s])
+
+    def rs_cross(s):
+        la, lb, full = lanes_of(REDUCE_SEGS[s])
+        wait(far2.at[:, :, full], recv.at[far2_sem[s]])
+        for a in range(2):
+            i, right, left, r, l, f = ring_of(1 - a)
+            for k, lanes, dev in ((r, la, right), (l, lb, left)):
+                pbuf[a, k, :, lanes] += far2[a, :, lanes]
+                remote(pbuf.at[a, k, :, lanes], dc2.at[1, a, :, lanes], dev, send_2, dc2_sem[s])
+
+    def rs_finish(s):
+        full = lanes_of(REDUCE_SEGS[s])[-1]
+        slots = 2 if RELAY_LAST[s] else 3
+        wait(dc2.at[:slots, :, :, full], recv.at[dc2_sem[s]])
+        for a in range(2):
+            acc = pbuf[a, cross[a], :, full]
+            for slot in range(slots):
+                acc = acc + dc2[slot, a, :, full]
+            gb[W * a:W * a + W, full] = acc
+
+    def rs_load(s):
+        t0, n, _ = REDUCE_SEGS[s]
+        rows = pl.ds(t0 * T, n * T)
+        wait(xown.at[rows], load_sem.at[x_load[s]])
+        wait(xown.at[rows], recv.at[swap_recv[s]])
+        lax.fori_loop(t0, t0 + n, transpose_in, 0)
+
+    def prepare(_):
         for c in small:
             c.wait()
         first = m_in[:, :HALF].astype(F32)
@@ -204,21 +247,11 @@
         fo[...] = jnp.where(on_first, c_in[:, :HALF], join_tail(r_out[...], c_in[:, HALF:], pad_c, pad_d))
 
     m_send, m_recv = next(sends), next(recvs)
-    n_segs = len(REDUCE_SEGS)
-    for t in range(n_segs + RING):
-        if t < n_segs:
-            t0, n, _ = REDUCE_SEGS[t]
-            rows = pl.ds(t0 * T, n * T)
-            wait(xown.at[rows], load_sem.at[x_load[t]])
-            wait(xown.at[rows], recv.at[swap_recv[t]])
-            lax.fori_loop(t0, t0 + n, transpose_in, 0)
-            rs_begin(t, 1)
-        if t == 1:
-            prepare()
-        for lag, work in enumerate((lambda s: rs_middle(s, 1), lambda s: (rs_end(s, 1), rs_begin(s, 2)), lambda s: rs_middle(s, 2), lambda s: rs_end(s, 2))):
-            s = t - 1 - lag
-            if 0 <= s < n_segs:
-                work(s)
+    def follow(plan, table):
+        for item in ",".join(plan).split(","):
+            table[item[0]](*(int(c) for c in item[1:]))
+
+    follow(REDUCE_PLAN, dict(S=rs_load, B=rs_begin, M=rs_middle, E=rs_end, C=rs_cross, F=rs_finish, H=prepare))
 
     lane = lax.broadcasted_iota(jnp.int32, (1, HALF), 1)
     is_in = lane >= jnp.where(on_first, 0, F_OUT)
@@ -275,57 +308,93 @@
     def total(v):
         return jnp.broadcast_to(sum_of(sum_of(v, 0), 1), (1, T))
 
-    qa[line_me] = jnp.concatenate([total(only_in(uu)), total(only_out(uu)), jnp.broadcast_to(f_out, (6, T))], axis=0)
-    qa_ref, qa_send, qa_recv = spread(qa, line_me, line)
+    pick = lax.broadcasted_iota(jnp.int32, (1, T), 1)
+    me_all = x * 32 + d
+    share = jnp.where(pick == 0, total(only_in(uu)), jnp.where(pick == 1, total(only_out(uu)), jnp.where(pick == 2, f_out / 16, jnp.where(pick == 3, sum_rows / 8, 0.0))))
+    qs[me_all] = share
+    q_send, q_recv = next(sends), next(recvs)
+
+    def tell(k, _):
+        other = lax.rem(me_all + k, 128)
+        remote(qs.at[me_all], qs.at[me_all], (lax.div(other, 32), lax.rem(other, 32)), q_send, q_recv)
+        return 0
+
+    lax.fori_loop(1, 128, tell, 0)
+    q_ref = qs.at[pl.ds(0, 127)]
     gb[...] = u
     fnew[...] = f_new
     f_send, f_recv = next(sends), next(recvs)
     remote(fnew, frecv, partner, f_send, f_recv)
-    wait(qa_ref, recv.at[qa_recv])
-    line_sum = jnp.sum(qa[...], axis=0)
-    qb[p] = jnp.concatenate([line_sum[:2], jnp.broadcast_to(sum_rows, (6, T))], axis=0)
-    qb_ref, qb_send, qb_recv = spread(qb, p, plane)
     wait(mx.at[0], recv.at[m_recv])
-    wait(qb_ref, recv.at[qb_recv])
-    plane_sum = jnp.sum(qb[...], axis=0)[:, :1]
-    mean_in = plane_sum[2:3] / D
-    mean_out = line_sum[2:3, :1] / N_OUT
-    rms_in = jnp.sqrt(plane_sum[:1] * mean_in / (D * N_IN))
-    rms_out = jnp.sqrt(plane_sum[1:2] * mean_out / (D * N_OUT))
+    wait(q_ref, recv.at[q_recv])
+    totals = jnp.sum(qs[...], axis=0)
+    mean_in = totals[:, 3:4] / D
+    mean_out = totals[:, 2:3] / N_OUT
+    rms_in = jnp.sqrt(totals[:, :1] * mean_in / (D * N_IN))
+    rms_out = jnp.sqrt(totals[:, 1:2] * mean_out / (D * N_OUT))
     scale = jnp.where(is_in, jnp.sqrt(mean_in) / jnp.maximum(1.0, rms_in), jnp.sqrt(mean_out) / jnp.maximum(1.0, rms_out))
 
     for a in range(2):
         t2buf[z, y, a] = (0.9 * mx[a] + 0.1 * (gb[W * a:W * a + W] * scale)).astype(BF16).astype(F32)
 
-    send_3, send_4 = next(sends), next(sends)
-    first_sem, rest_sem, first2_sem, rest2_sem = ([next(recvs) for _ in GATHER_SEGS] for _ in range(4))
-
-    def ag_refs(phase):
-        if phase == 1:
-            return (lambda a, k, lanes: t2buf.at[k, y, 0, :, lanes] if a == 0 else t2buf.at[z, k, 1, :, lanes]), send_3, first_sem, rest_sem
-        return (lambda a, k, lanes: chunk(t2buf, a, k, lanes)), send_4, first2_sem, rest2_sem
-
-    def ag_begin(s, phase):
+    send_3 = next(sends)
+    a1_first, a1_rest, a1_fwd, a2_rest = ([next(recvs) for _ in GATHER_SEGS] for _ in range(4))
+    a2_first = [[next(recvs) for _ in u] for u in GATHER_UNITS]
+
+    def swap_around(ref, ring_a, s, first, rest):
         la, lb, _ = lanes_of(GATHER_SEGS[s])
-        ref, ss, fs, rs = ag_refs(phase)
-        for lanes_r, lanes_l, sem in ((la, lb, fs[s]), (lb, la, rs[s])):
+        for lanes_r, lanes_l, sem in ((la, lb, first), (lb, la, rest)):
             for a in range(2):
-                i, right, left, r, l, f = rs_ring(a, 3 - phase)
-                remote(ref(a, i, lanes_r), ref(a, i, lanes_r), right, ss, sem)
-                remote(ref(a, i, lanes_l), ref(a, i, lanes_l), left, ss, sem)
-
-    def ag_middle(s, phase):
-        la, lb, full = lanes_of(GATHER_SEGS[s])
-        ref, ss, fs, rs = ag_refs(phase)
-        wait((far2.at[:, :, full] if phase == 1 else far.at[:, :, :, full]), recv.at[fs[s]])
-        for a in range(2):
-            i, right, left, r, l, f = rs_ring(a, 3 - phase)
-            remote(ref(a, l, la), ref(a, l, la), right, ss, rs[s])
-            remote(ref(a, r, lb), ref(a, r, lb), left, ss, rs[s])
-
-    def ag_end(s, phase):
-        full = lanes_of(GATHER_SEGS[s])[-1]
-        wait((dc2.at[:, :, :, full] if phase == 1 else dc.at[:, :, :, :, full]), recv.at[ag_refs(phase)[-1][s]])
+                i, right, left, r, l, f = ring_of(ring_a(a))
+                for src in ref(a, i, lanes_r):
+                    remote(src, src, right, send_3, sem)
+                for src in ref(a, i, lanes_l):
+                    remote(src, src, left, send_3, sem)
+
+    def pass_on(ref, ring_a, s, sem):
+        la, lb, _ = lanes_of(GATHER_SEGS[s])
+        for a in range(2):
+            i, right, left, r, l, f = ring_of(ring_a(a))
+            for src in ref(a, l, la):
+                remote(src, src, right, send_3, sem)
+            for src in ref(a, r, lb):
+                remote(src, src, left, send_3, sem)
+
+    def one_ref(a, q, lanes):
+        return [piece(t2buf, a, ring_of(a)[0], q, lanes)]
+
+    def two_ref(s, u):
+        offs = GATHER_UNITS[s][u]
+        return lambda a, k, lanes: [piece(t2buf, a, k, block(a, o), lanes) for o in (offs or (None,))]
+
+    def same(a):
+        return a
+
+    def other(a):
+        return 1 - a
+
+    def a1_begin(s):
+        swap_around(one_ref, other, s, a1_first[s], a1_rest[s])
+
+    def a2_begin(s, u):
+        swap_around(two_ref(s, u), same, s, a2_first[s][u], a2_rest[s])
+
+    def a1_middle(s):
+        wait(far2.at[:, :, lanes_of(GATHER_SEGS[s])[-1]], recv.at[a1_first[s]])
+        pass_on(one_ref, other, s, a1_fwd[s])
+
+    def a1_near(s):
+        wait(far2.at[:, :, lanes_of(GATHER_SEGS[s])[-1]], recv.at[a1_rest[s]])
+
+    def a1_far(s):
+        wait(far2.at[:, :, lanes_of(GATHER_SEGS[s])[-1]], recv.at[a1_fwd[s]])
+
+    def a2_middle(s, u):
+        wait(far.at[:, :len(GATHER_UNITS[s][u] or BLOCKS), :, lanes_of(GATHER_SEGS[s])[-1]], recv.at[a2_first[s][u]])
+        pass_on(two_ref(s, u), same, s, a2_rest[s])
+
+    def a2_end(s):
+        wait(dc.at[:, :, :, :, lanes_of(GATHER_SEGS[s])[-1]], recv.at[a2_rest[s]])
 
     lr_wd = lr * wd
     base = core * HALF
@@ -344,7 +413,6 @@
     out_send, out_recv = next(sends), next(recvs)
 
     def state_out():
-        remote(t2buf.at[z, y, 1 - core], mrecv, partner, mo_send, mo_recv)
         wait(frecv, recv.at[f_recv])
         wait(mrecv, recv.at[mo_recv])
         for mine, theirs, out_in, out_out in ((t2buf[z, y, core], mrecv[...], o_m_in, o_m_out), (fnew[...], frecv[...], o_c_in, o_r_out)):
@@ -359,26 +427,20 @@
         wait(wown, load_sem.at[w_load])
 
     def finish(s):
-        ag_end(s, 2)
+        if s == 0:
+            state_out()
+        a2_end(s)
         t0, n, _ = GATHER_SEGS[s]
         lax.fori_loop(t0, t0 + n, transpose_out, 0)
         span = pl.ds(pl.multiple_of(base + t0 * T, T), n * T)
         remote(o_w.at[span], o_w.at[span], partner, out_send, out_recv)
 
-    n_segs = len(GATHER_SEGS)
-    for t in range(n_segs + RING):
-        if t < n_segs:
-            ag_begin(t, 1)
-        if t == 3:
-            state_out()
-        for lag, work in enumerate((lambda s: ag_middle(s, 1), lambda s: (ag_end(s, 1), ag_begin(s, 2)), lambda s: ag_middle(s, 2), finish)):
-            s = t - 1 - lag
-            if 0 <= s < n_segs:
-                work(s)
+    remote(t2buf.at[z, y, 1 - core], mrecv, partner, mo_send, mo_recv)
+    follow(GATHER_PLAN, dict(A=a1_begin, B=a2_begin, M=a1_middle, N=a1_near, W=a1_far, P=a2_middle, F=finish))
 
     wait(xown, recv.at[out_recv])
-    for ref, sem in ((xown, swap_send), (ms, m_send), (tbuf.at[:3], send_1), (tbuf.at[0, :3], send_2), (fv_ref, fv_send), (rv_ref, rv_send), (qa_ref, qa_send), (qb_ref, qb_send),
-                     (fnew, f_send), (t2buf.at[0, :3], send_3), (t2buf.at[:3], send_4), (ms, mo_send), (xown, out_send)):
+    for ref, sem in ((xown, swap_send), (ms, m_send), (tbuf.at[:3], send_1), (tbuf.at[0, :3], send_2), (fv_ref, fv_send), (rv_ref, rv_send), (q_ref, q_send),
+                     (fnew, f_send), (xown.at[pl.ds(0, HALF - HALF // 16)], send_3), (ms, mo_send), (xown, out_send)):
         wait(ref, send.at[sem])
 
 
@@ -412,9 +474,9 @@
         out_specs=(vmem,) * (1 + len(small)),
         scratch_shapes=[
             *in_vmem, buf(*half), buf(*half), buf(*half), buf(*whole), buf(*whole),
-            buf(2, RING, *part), buf(2, 2, RING, *part), buf(2, RING, *part), buf(2, *part), buf(2, 2, *part),
+            buf(2, RING, *part), buf(2, 2, RING, *part), buf(2, RING, *part), buf(2, *part), buf(3, 2, *part),
             buf(2, *part), buf(*part), buf(*part), buf(*line), buf(*line), buf(*line),
-            buf(16, *line), buf(8, 8, T), buf(8, 8, T), buf(16, 8, T),
+            buf(16, *line), buf(8, 8, T), buf(128, 1, T),
             buf(2 * W, HALF), buf(W, T), buf(W, 2 * T), buf(1, T), buf(1, 2 * T), buf(8, T),
             pltpu.SemaphoreType.DMA((N_LOAD,)), pltpu.SemaphoreType.DMA((N_SEND,)), pltpu.SemaphoreType.DMA((N_RECV,)),
         ],

time: 83.7 us -> 75.7 us (0.904)
  Pallas kernels: 81 us -> 73 us
    pallas_call x1, Pallas kernels: 77.9 us -> 70 us  [call(): pl.pallas_call(kernel, name='adafactor_step', out_shape=(buf(2 * HALF, D)...]
where the time goes in v4:
time: 75.7 us; the launch traced here: 75.6 us
  Pallas kernels  73 us (96%)
  between operations  2.58 us (3%)
    pallas_call x1, Pallas kernels, call(): pl.pallas_call(kernel, name='adafactor_step', out_shape=(buf(2 * HALF, D)...  70 us
    pallas_call x1, Pallas kernels, call(): pl.pallas_call(store_kernel, name='store_outputs', out_shape=tuple((jax.S...  3.04 us

profile of v4, /device:TPU:1, one launch (start us, length us, event | category | flops | bytes accessed | tf_op | source)
XLA Modules:
  0.0 75.6 jit_solution(1111952558495864467)
XLA Ops:
  2.6 70.0 %adafactor_step.1 = (f32[2304,768]{1,0:T(8,128)S(1)}, bf16[24,1344]{1,0:T(8,128)(2,1)S(1)}, bf16[24,960]{1,0:T(8,128)(2,1)S(1)}, f32[1,24]{1,0:T(1,128)S(1)}, f3...) custom-call(f32[1]{0:T(128)} %bitcast.23.lr_ref, f32[1]{0:T(128)} %bitcast.24.wd_ref, ...), custom_call_target="tpu_custom_call" | custom-call | tf_op jit(solution)/shard_map/adafactor_step/pallas_call | solution.py:469
  72.5 3.0 %store_outputs.1 = (f32[1344,768]{1,0:T(8,128)}, f32[960,768]{1,0:T(8,128)}, bf16[24,1344]{1,0:T(8,128)(2,1)}, bf16[24,960]{1,0:T(8,128)(2,1)}, f32[1,24]{1,0:T(...) custom-call(f32[2304,768]{1,0:T(8,128)S(1)} %get-tuple-element.23.w, ...), custom_call_target="tpu_custom_call" | custom-call | tf_op jit(solution)/shard_map/store_outputs/pallas_call | solution.py:485

commit v5 on v4

--- a/solution.py
+++ b/solution.py
@@ -28,6 +28,7 @@
 RELAY_LAST = (True, False, False)
 REDUCE_PLAN = ("S0,B00,S1,B10,M00,S2,B20,B21,B22,B23,H0,M10,E00", "M20,M21,M22,M23,E10,C0,E20,E21,E22,E23,F1,F0,F2")
 GATHER_PLAN = ("A0,B00,A1,A2,M0,N0,B01,P00,M1,N1,M2,N2,W0,B02,B10,B11", "P01,W1,W2,B12,P02,P10,B20,P11,P12,F0,P20,F1,F2")
+FAR_FIRST = (2, 1, 3, 0)
 ROWS_ONE = pl.ds(0, 1)
 N_SEND = 11
 N_RECV = 45
@@ -76,8 +77,10 @@
     def at(xx, pp, cc):
         return (xx, pp * 2 + cc)
 
+    turn = 1 + 2 * core
+
     def step(i, k):
-        return lax.rem(i + k, RING)
+        return lax.rem(i + k * turn, RING)
 
     partner = at(x, p, 1 - core)
     sends = iter(range(N_SEND))
@@ -113,7 +116,7 @@
     for k in range(1, 8):
         other = lax.rem(line_me + k, 8)
         line.append(at(lax.div(other, 2), p, lax.rem(other, 2)))
-    plane = [at(x, lax.rem(p + k, 16), core) for k in range(1, 16)]
+    plane = [at(x, step(z, i) * RING + step(y, k), core) for i in FAR_FIRST for k in FAR_FIRST if i or k]
     greet = [dev for _, right, left, _ in ring for dev in (right, left)] + line
     for dev in greet:
         pl.semaphore_signal(barrier, inc=1, device_id=dev, device_id_type=MESH)
@@ -315,11 +318,18 @@
     q_send, q_recv = next(sends), next(recvs)
 
     def tell(k, _):
-        other = lax.rem(me_all + k, 128)
-        remote(qs.at[me_all], qs.at[me_all], (lax.div(other, 32), lax.rem(other, 32)), q_send, q_recv)
+        chip = lax.rem(z + 6 - lax.div(k, RING), RING) * RING + lax.rem(y + 6 - lax.rem(k, RING), RING)
+        for i in FAR_FIRST:
+            for c in (1 - core, core):
+                def go():
+                    remote(qs.at[me_all], qs.at[me_all], at(lax.rem(x + i, RING), chip, c), q_send, q_recv)
+                if i == 0 and c is core:
+                    pl.when(k != 10)(go)
+                else:
+                    go()
         return 0
 
-    lax.fori_loop(1, 128, tell, 0)
+    lax.fori_loop(0, 16, tell, 0)
     q_ref = qs.at[pl.ds(0, 127)]
     gb[...] = u
     fnew[...] = f_new
@@ -431,9 +441,14 @@
             state_out()
         a2_end(s)
         t0, n, _ = GATHER_SEGS[s]
-        lax.fori_loop(t0, t0 + n, transpose_out, 0)
-        span = pl.ds(pl.multiple_of(base + t0 * T, T), n * T)
-        remote(o_w.at[span], o_w.at[span], partner, out_send, out_recv)
+
+        def tile(j, _):
+            transpose_out(j, 0)
+            span = pl.ds(pl.multiple_of(base + j * T, T), T)
+            remote(o_w.at[span], o_w.at[span], partner, out_send, out_recv)
+            return 0
+
+        lax.fori_loop(t0, t0 + n, tile, 0)
 
     remote(t2buf.at[z, y, 1 - core], mrecv, partner, mo_send, mo_recv)
     follow(GATHER_PLAN, dict(A=a1_begin, B=a2_begin, M=a1_middle, N=a1_near, W=a1_far, P=a2_middle, F=finish))
@@ -445,8 +460,9 @@
 
 
 def store_kernel(w, m_in, m_out, r_in, c_in, r_out, c_out, o_w_in, o_w_out, o_m_in, o_m_out, o_r_in, o_c_in, o_r_out, o_c_out, sem):
-    pairs = [(w.at[pl.ds(0, HALF)], o_w_in.at[pl.ds(0, HALF)]), (w.at[pl.ds(HALF, F_OUT)], o_w_out), (w.at[pl.ds(HALF + F_OUT, TAIL)], o_w_in.at[pl.ds(HALF, TAIL)]),
-             (m_in, o_m_in), (m_out, o_m_out), (r_in, o_r_in), (c_in, o_c_in), (r_out, o_r_out), (c_out, o_c_out)]
+    pairs = [(w.at[pl.ds(src + k * rows, rows)], out.at[pl.ds(dst + k * rows, rows)]) for src, out, dst, rows, count in (
+        (0, o_w_in, 0, TAIL, 6), (HALF, o_w_out, 0, TAIL, 5), (HALF + F_OUT, o_w_in, HALF, TAIL, 1)) for k in range(count)]
+    pairs += [(m_in, o_m_in), (m_out, o_m_out), (r_in, o_r_in), (c_in, o_c_in), (r_out, o_r_out), (c_out, o_c_out)]
     work = [pltpu.make_async_copy(src, dst, sem.at[n]) for n, (src, dst) in enumerate(pairs)]
     for c in work:
         c.start()
@@ -488,7 +504,7 @@
         out_shape=tuple(jax.ShapeDtypeStruct(*a) for a in (((F_IN, D), F32), ((F_OUT, D), F32), *small)),
         in_specs=[vmem] * (1 + len(small)),
         out_specs=(hbm,) * (2 + len(small)),
-        scratch_shapes=[pltpu.SemaphoreType.DMA((9,))],
+        scratch_shapes=[pltpu.SemaphoreType.DMA((18,))],
         compiler_params=pltpu.CompilerParams(vmem_limit_bytes=16 << 20),
     )(*held)
 

time: 75.7 us -> 74 us (0.978)
  Pallas kernels: 73 us -> 71.3 us
    pallas_call x1, Pallas kernels: 70 us -> 68.3 us  [call(): pl.pallas_call(kernel, name='adafactor_step', out_shape=(buf(2 * HALF, D)...]
where the time goes in v5:
time: 74 us; the launch traced here: 73.9 us
  Pallas kernels  71.3 us (96%)
  between operations  2.58 us (3%)
    pallas_call x1, Pallas kernels, call(): pl.pallas_call(kernel, name='adafactor_step', out_shape=(buf(2 * HALF, D)...  68.3 us
    pallas_call x1, Pallas kernels, call(): pl.pallas_call(store_kernel, name='store_outputs', out_shape=tuple((jax.S...  3.07 us

profile of v5, /device:TPU:1, one launch (start us, length us, event | category | flops | bytes accessed | tf_op | source)
XLA Modules:
  0.0 73.9 jit_solution(18323880007536700295)
XLA Ops:
  2.6 68.3 %adafactor_step.1 = (f32[2304,768]{1,0:T(8,128)S(1)}, bf16[24,1344]{1,0:T(8,128)(2,1)S(1)}, bf16[24,960]{1,0:T(8,128)(2,1)S(1)}, f32[1,24]{1,0:T(1,128)S(1)}, f3...) custom-call(f32[1]{0:T(128)} %bitcast.23.lr_ref, f32[1]{0:T(128)} %bitcast.24.wd_ref, ...), custom_call_target="tpu_custom_call" | custom-call | tf_op jit(solution)/shard_map/adafactor_step/pallas_call | solution.py:485
  70.8 3.1 %store_outputs.1 = (f32[1344,768]{1,0:T(8,128)}, f32[960,768]{1,0:T(8,128)}, bf16[24,1344]{1,0:T(8,128)(2,1)}, bf16[24,960]{1,0:T(8,128)(2,1)}, f32[1,24]{1,0:T(...) custom-call(f32[2304,768]{1,0:T(8,128)S(1)} %get-tuple-element.23.w, ...), custom_call_target="tpu_custom_call" | custom-call | tf_op jit(solution)/shard_map/store_outputs/pallas_call | solution.py:501

commit v6 on v5

--- a/solution.py
+++ b/solution.py
@@ -21,17 +21,21 @@
 W = 24
 RING = 4
 REDUCE_SEGS = ((0, 2, 1), (2, 2, 1), (4, 5, 2))
-GATHER_SEGS = ((0, 3, 2), (3, 4, 2), (7, 2, 1))
+EARLY = 2
+GATHER_SEGS = ((0, 2, 1), (0, 2, 1), (2, 3, 2), (5, 2, 1), (7, 2, 1))
+BLOCKS = (0, 1, 3, 2)
+SPLIT = ((0,), (1, 3), (2,))
+GATHER_UNITS = (SPLIT, SPLIT, SPLIT, SPLIT, (None,))
 REDUCE_UNITS = ((None,), (None,), (2, 1, 3, 0))
-BLOCKS = (0, 1, 3, 2)
-GATHER_UNITS = (((0,), (1, 3), (2,)), ((0,), (1, 3), (2,)), (None,))
 RELAY_LAST = (True, False, False)
-REDUCE_PLAN = ("S0,B00,S1,B10,M00,S2,B20,B21,B22,B23,H0,M10,E00", "M20,M21,M22,M23,E10,C0,E20,E21,E22,E23,F1,F0,F2")
-GATHER_PLAN = ("A0,B00,A1,A2,M0,N0,B01,P00,M1,N1,M2,N2,W0,B02,B10,B11", "P01,W1,W2,B12,P02,P10,B20,P11,P12,F0,P20,F1,F2")
+REDUCE_PLAN = ("S0,B00,S1,B10,M00,S2,B20,B21,B22,B23,H0,M10,E00", "M20,M21,M22,M23,E10,C0,E20,E21,K0,E22,E23,a1,b10,F1,F0,F2")
+EARLY_PLAN = ("M1,N1,B11,P10,A0,B00,W1,B12,P11",)
+EARLY_PLAN_END = ("M0,N0,B01,P00,P12,W0,B02,P01",)
+GATHER_PLAN = ("A2,B20,A3,A4,P02,M2,N2,B21,P20,M3,N3,M4,N4,W2,B22,F0", "B30,B31,P21,W3,B32,W4,B40,P22,P30,P31,P32,P40,F2,F3,F4")
 FAR_FIRST = (2, 1, 3, 0)
 ROWS_ONE = pl.ds(0, 1)
 N_SEND = 11
-N_RECV = 45
+N_RECV = 59
 N_LOAD = 10
 
 
@@ -62,7 +66,7 @@
 def kernel(lr_ref, wd_ref, beta_ref, g_in, g_out, w_in, w_out, h_m_in, h_m_out, h_r_in, h_c_in, h_r_out, h_c_out,
            o_w, o_m_in, o_m_out, o_r_in, o_c_in, o_r_out, o_c_out,
            m_in, m_out, r_in, c_in, r_out, c_out,
-           xown, xrecv, wown, tbuf, t2buf, far, dc, pbuf, far2, dc2,
+           xown, xrecv, wown, tbuf, t2buf, m2buf, mnew, rf, colv, far, dc, pbuf, far2, dc2,
            mx, ms, mrecv, fo, fnew, frecv, fv, rv, qs, gb, pad_a, pad_b, pad_c, pad_d, rowpad,
            load_sem, send, recv):
     x = lax.axis_index("tp")
@@ -250,11 +254,84 @@
         fo[...] = jnp.where(on_first, c_in[:, :HALF], join_tail(r_out[...], c_in[:, HALF:], pad_c, pad_d))
 
     m_send, m_recv = next(sends), next(recvs)
+    send_3 = next(sends)
+    a1_first, a1_rest, a1_fwd, a2_rest = ([next(recvs) for _ in GATHER_SEGS] for _ in range(4))
+    a2_first = [[next(recvs) for _ in u] for u in GATHER_UNITS]
+
+    def swap_around(ref, ring_a, s, first, rest):
+        la, lb, _ = lanes_of(GATHER_SEGS[s])
+        for lanes_r, lanes_l, sem in ((la, lb, first), (lb, la, rest)):
+            for a in range(2):
+                i, right, left, r, l, f = ring_of(ring_a(a))
+                for src in ref(a, i, lanes_r):
+                    remote(src, src, right, send_3, sem)
+                for src in ref(a, i, lanes_l):
+                    remote(src, src, left, send_3, sem)
+
+    def pass_on(ref, ring_a, s, sem):
+        la, lb, _ = lanes_of(GATHER_SEGS[s])
+        for a in range(2):
+            i, right, left, r, l, f = ring_of(ring_a(a))
+            for src in ref(a, l, la):
+                remote(src, src, right, send_3, sem)
+            for src in ref(a, r, lb):
+                remote(src, src, left, send_3, sem)
+
+    def store_of(s):
+        return m2buf if s == 1 else t2buf
+
+    def one_ref(s):
+        return lambda a, q, lanes: [piece(store_of(s), a, ring_of(a)[0], q, lanes)]
+
+    def two_ref(s, u):
+        offs = GATHER_UNITS[s][u]
+        return lambda a, k, lanes: [piece(store_of(s), a, k, block(a, o), lanes) for o in (offs or (None,))]
+
+    def same(a):
+        return a
+
+    def other(a):
+        return 1 - a
+
+    def a1_begin(s):
+        swap_around(one_ref(s), other, s, a1_first[s], a1_rest[s])
+
+    def a2_begin(s, u):
+        swap_around(two_ref(s, u), same, s, a2_first[s][u], a2_rest[s])
+
+    def a1_middle(s):
+        wait(far2.at[:, :, lanes_of(GATHER_SEGS[s])[-1]], recv.at[a1_first[s]])
+        pass_on(one_ref(s), other, s, a1_fwd[s])
+
+    def a1_near(s):
+        wait(far2.at[:, :, lanes_of(GATHER_SEGS[s])[-1]], recv.at[a1_rest[s]])
+
+    def a1_far(s):
+        wait(far2.at[:, :, lanes_of(GATHER_SEGS[s])[-1]], recv.at[a1_fwd[s]])
+
+    def a2_middle(s, u):
+        wait(far.at[:, :len(GATHER_UNITS[s][u] or BLOCKS), :, lanes_of(GATHER_SEGS[s])[-1]], recv.at[a2_first[s][u]])
+        pass_on(two_ref(s, u), same, s, a2_rest[s])
+
+    def a2_end(s):
+        wait(dc.at[:, :, :, :, lanes_of(GATHER_SEGS[s])[-1]], recv.at[a2_rest[s]])
+
+    def gather(plan, **more):
+        follow(plan, dict(A=a1_begin, B=a2_begin, M=a1_middle, N=a1_near, W=a1_far, P=a2_middle, **more))
+
+    early = pl.ds(0, EARLY * T)
+    late = pl.ds(EARLY * T, HALF - EARLY * T)
+
+    def keep(_):
+        wait(mx.at[0], recv.at[m_recv])
+        for a in range(2):
+            m2buf[z, y, a] = mx[a, :, early]
+
     def follow(plan, table):
         for item in ",".join(plan).split(","):
             table[item[0]](*(int(c) for c in item[1:]))
 
-    follow(REDUCE_PLAN, dict(S=rs_load, B=rs_begin, M=rs_middle, E=rs_end, C=rs_cross, F=rs_finish, H=prepare))
+    follow(REDUCE_PLAN, dict(S=rs_load, B=rs_begin, M=rs_middle, E=rs_end, C=rs_cross, F=rs_finish, H=prepare, K=keep, a=a1_begin, b=a2_begin))
 
     lane = lax.broadcasted_iota(jnp.int32, (1, HALF), 1)
     is_in = lane >= jnp.where(on_first, 0, F_OUT)
@@ -295,6 +372,9 @@
     rv_ref, rv_send, rv_recv = spread(rv, line_me, line)
 
     lr, wd, beta = lr_ref[0], wd_ref[0], beta_ref[0]
+    for a in range(2):
+        t2buf[z, y, a, :, early] = gb[W * a:W * a + W, early]
+    gather(EARLY_PLAN)
     wait(rv_ref, recv.at[rv_recv])
     row_sum = jnp.sum(rv[...], axis=0)
     row_old = rv[0] + rv[1]
@@ -304,7 +384,8 @@
     sum_rows = sum_of(r_new, 1)
     wait(fv_ref, recv.at[fv_recv])
     f_new = beta * fo[...] + (1.0 - beta) * (jnp.sum(fv[...], axis=0) / D)
-    u = v * (1.0 / jnp.sqrt(f_new))
+    col_scale = 1.0 / jnp.sqrt(f_new)
+    u = v * col_scale
     uu = u * u
     f_out = sum_of(only_out(f_new), 1)
 
@@ -313,7 +394,8 @@
 
     pick = lax.broadcasted_iota(jnp.int32, (1, T), 1)
     me_all = x * 32 + d
-    share = jnp.where(pick == 0, total(only_in(uu)), jnp.where(pick == 1, total(only_out(uu)), jnp.where(pick == 2, f_out / 16, jnp.where(pick == 3, sum_rows / 8, 0.0))))
+    share = jnp.where(pick == 0, total(only_in(uu)), jnp.where(pick == 1, total(only_out(uu)), jnp.where(pick == 2, f_out / 16, sum_rows / 8)))
+    share = jnp.where(pick < 16, share, pltpu.roll(jnp.where(on_first, r_new, c_new), 16, 1))
     qs[me_all] = share
     q_send, q_recv = next(sends), next(recvs)
 
@@ -335,7 +417,8 @@
     fnew[...] = f_new
     f_send, f_recv = next(sends), next(recvs)
     remote(fnew, frecv, partner, f_send, f_recv)
-    wait(mx.at[0], recv.at[m_recv])
+    colv[ROWS_ONE] = col_scale
+    gather(EARLY_PLAN_END)
     wait(q_ref, recv.at[q_recv])
     totals = jnp.sum(qs[...], axis=0)
     mean_in = totals[:, 3:4] / D
@@ -345,79 +428,31 @@
     scale = jnp.where(is_in, jnp.sqrt(mean_in) / jnp.maximum(1.0, rms_in), jnp.sqrt(mean_out) / jnp.maximum(1.0, rms_out))
 
     for a in range(2):
-        t2buf[z, y, a] = (0.9 * mx[a] + 0.1 * (gb[W * a:W * a + W] * scale)).astype(BF16).astype(F32)
-
-    send_3 = next(sends)
-    a1_first, a1_rest, a1_fwd, a2_rest = ([next(recvs) for _ in GATHER_SEGS] for _ in range(4))
-    a2_first = [[next(recvs) for _ in u] for u in GATHER_UNITS]
-
-    def swap_around(ref, ring_a, s, first, rest):
-        la, lb, _ = lanes_of(GATHER_SEGS[s])
-        for lanes_r, lanes_l, sem in ((la, lb, first), (lb, la, rest)):
-            for a in range(2):
-                i, right, left, r, l, f = ring_of(ring_a(a))
-                for src in ref(a, i, lanes_r):
-                    remote(src, src, right, send_3, sem)
-                for src in ref(a, i, lanes_l):
-                    remote(src, src, left, send_3, sem)
-
-    def pass_on(ref, ring_a, s, sem):
-        la, lb, _ = lanes_of(GATHER_SEGS[s])
-        for a in range(2):
-            i, right, left, r, l, f = ring_of(ring_a(a))
-            for src in ref(a, l, la):
-                remote(src, src, right, send_3, sem)
-            for src in ref(a, r, lb):
-                remote(src, src, left, send_3, sem)
-
-    def one_ref(a, q, lanes):
-        return [piece(t2buf, a, ring_of(a)[0], q, lanes)]
-
-    def two_ref(s, u):
-        offs = GATHER_UNITS[s][u]
-        return lambda a, k, lanes: [piece(t2buf, a, k, block(a, o), lanes) for o in (offs or (None,))]
-
-    def same(a):
-        return a
-
-    def other(a):
-        return 1 - a
-
-    def a1_begin(s):
-        swap_around(one_ref, other, s, a1_first[s], a1_rest[s])
-
-    def a2_begin(s, u):
-        swap_around(two_ref(s, u), same, s, a2_first[s][u], a2_rest[s])
-
-    def a1_middle(s):
-        wait(far2.at[:, :, lanes_of(GATHER_SEGS[s])[-1]], recv.at[a1_first[s]])
-        pass_on(one_ref, other, s, a1_fwd[s])
-
-    def a1_near(s):
-        wait(far2.at[:, :, lanes_of(GATHER_SEGS[s])[-1]], recv.at[a1_rest[s]])
-
-    def a1_far(s):
-        wait(far2.at[:, :, lanes_of(GATHER_SEGS[s])[-1]], recv.at[a1_fwd[s]])
-
-    def a2_middle(s, u):
-        wait(far.at[:, :len(GATHER_UNITS[s][u] or BLOCKS), :, lanes_of(GATHER_SEGS[s])[-1]], recv.at[a2_first[s][u]])
-        pass_on(two_ref(s, u), same, s, a2_rest[s])
-
-    def a2_end(s):
-        wait(dc.at[:, :, :, :, lanes_of(GATHER_SEGS[s])[-1]], recv.at[a2_rest[s]])
+        mnew[a] = (0.9 * mx[a] + 0.1 * (gb[W * a:W * a + W] * scale)).astype(BF16).astype(F32)
+        t2buf[z, y, a, :, late] = mnew[a, :, late]
 
     lr_wd = lr * wd
     base = core * HALF
 
-    def transpose_out(j, _):
+    def put_rows(j, tiles):
+        dest = pl.ds(pl.multiple_of(base + j * T, T), T)
         rows = pl.ds(pl.multiple_of(j * T, T), T)
-        dest = pl.ds(pl.multiple_of(base + j * T, T), T)
         for h in range(2):
             cols = pl.ds(h * D // 2, D // 2)
-            t = jnp.concatenate([t2buf[2 * h + zz, yy, a, :, rows] for zz, yy, a in blocks], axis=0)
             w = wown[rows, cols]
-            o_w[dest, cols] = w - lr * t.T - lr_wd * w
-        return 0
+            o_w[dest, cols] = w - lr * jnp.concatenate(tiles(h, rows), axis=0).T - lr_wd * w
+        remote(o_w.at[dest], o_w.at[dest], partner, out_send, out_recv)
+
+    def moments(h, rows):
+        return [t2buf[2 * h + zz, yy, a, :, rows] for zz, yy, a in blocks]
+
+    def moments_early(h, rows):
+        out = []
+        for zz, yy, a in blocks:
+            where = (2 * h + zz, yy, a, ALL, rows)
+            upd = t2buf[where] * rf[(2 * h + zz) * RING + yy, W * a:W * a + W] * colv[ROWS_ONE, rows] * colv[pl.ds(1, 1), rows]
+            out.append((0.9 * m2buf[where] + 0.1 * upd).astype(BF16).astype(F32))
+        return out
 
     mo_send, mo_recv = next(sends), next(recvs)
     out_send, out_recv = next(sends), next(recvs)
@@ -425,7 +460,7 @@
     def state_out():
         wait(frecv, recv.at[f_recv])
         wait(mrecv, recv.at[mo_recv])
-        for mine, theirs, out_in, out_out in ((t2buf[z, y, core], mrecv[...], o_m_in, o_m_out), (fnew[...], frecv[...], o_c_in, o_r_out)):
+        for mine, theirs, out_in, out_out in ((mnew[core], mrecv[...], o_m_in, o_m_out), (fnew[...], frecv[...], o_c_in, o_r_out)):
             lo = jnp.where(on_first, mine, theirs)
             hi = jnp.where(on_first, theirs, mine)
             out_in[:, :HALF] = lo.astype(out_in.dtype)
@@ -434,28 +469,37 @@
         for new, out in ((r_new, o_r_in), (c_new, o_c_out)):
             rowpad[...] = jnp.broadcast_to(new, rowpad.shape)
             out[...] = jnp.where(on_first, rowpad[...], pltpu.roll(rowpad[...], T - W, 1))[:1, :W]
-        wait(wown, load_sem.at[w_load])
 
     def finish(s):
         if s == 0:
+            wait(wown, load_sem.at[w_load])
+            colv[pl.ds(1, 1)] = scale
+            shifted = lax.broadcasted_iota(jnp.int32, (2 * W, T), 0) + 16 == lax.broadcasted_iota(jnp.int32, (2 * W, T), 1)
+
+            def row_factor(chip, _):
+                col = sum_of(jnp.where(shifted, qs[x * 32 + chip * 2 + core], 0.0), 1)
+                rf[chip] = jnp.broadcast_to(1.0 / jnp.sqrt(col), (2 * W, T))
+                return 0
+
+            lax.fori_loop(0, 16, row_factor, 0)
+            a2_end(1)
+        if s == 2:
             state_out()
         a2_end(s)
         t0, n, _ = GATHER_SEGS[s]
 
         def tile(j, _):
-            transpose_out(j, 0)
-            span = pl.ds(pl.multiple_of(base + j * T, T), T)
-            remote(o_w.at[span], o_w.at[span], partner, out_send, out_recv)
+            put_rows(j, moments if s else moments_early)
             return 0
 
         lax.fori_loop(t0, t0 + n, tile, 0)
 
-    remote(t2buf.at[z, y, 1 - core], mrecv, partner, mo_send, mo_recv)
-    follow(GATHER_PLAN, dict(A=a1_begin, B=a2_begin, M=a1_middle, N=a1_near, W=a1_far, P=a2_middle, F=finish))
+    remote(mnew.at[1 - core], mrecv, partner, mo_send, mo_recv)
+    gather(GATHER_PLAN, F=finish)
 
     wait(xown, recv.at[out_recv])
     for ref, sem in ((xown, swap_send), (ms, m_send), (tbuf.at[:3], send_1), (tbuf.at[0, :3], send_2), (fv_ref, fv_send), (rv_ref, rv_send), (q_ref, q_send),
-                     (fnew, f_send), (xown.at[pl.ds(0, HALF - HALF // 16)], send_3), (ms, mo_send), (xown, out_send)):
+                     (fnew, f_send), (o_w.at[pl.ds(0, (HALF + EARLY * T) * 15 // 16)], send_3), (ms, mo_send), (xown, out_send)):
         wait(ref, send.at[sem])
 
 
@@ -489,7 +533,7 @@
         in_specs=[smem] * 3 + [hbm] * (len(args) - 3),
         out_specs=(vmem,) * (1 + len(small)),
         scratch_shapes=[
-            *in_vmem, buf(*half), buf(*half), buf(*half), buf(*whole), buf(*whole),
+            *in_vmem, buf(*half), buf(*half), buf(*half), buf(*whole), buf(*whole), buf(RING, RING, 2, W, EARLY * T), buf(2, *part), buf(16, 2 * W, T), buf(8, HALF),
             buf(2, RING, *part), buf(2, 2, RING, *part), buf(2, RING, *part), buf(2, *part), buf(3, 2, *part),
             buf(2, *part), buf(*part), buf(*part), buf(*line), buf(*line), buf(*line),
             buf(16, *line), buf(8, 8, T), buf(128, 1, T),

time: 74 us -> 72 us (0.973)
  Pallas kernels: 71.3 us -> 69.3 us
    pallas_call x1, Pallas kernels: 68.3 us -> 66.3 us  [call(): pl.pallas_call(kernel, name='adafactor_step', out_shape=(buf(2 * HALF, D)...]
where the time goes in v6:
time: 72 us; the launch traced here: 71.9 us
  Pallas kernels  69.3 us (96%)
  between operations  2.58 us (4%)
    pallas_call x1, Pallas kernels, call(): pl.pallas_call(kernel, name='adafactor_step', out_shape=(buf(2 * HALF, D)...  66.3 us
    pallas_call x1, Pallas kernels, call(): pl.pallas_call(store_kernel, name='store_outputs', out_shape=tuple((jax.S...  3.07 us

profile of v6, /device:TPU:1, one launch (start us, length us, event | category | flops | bytes accessed | tf_op | source)
XLA Modules:
  0.0 71.9 jit_solution(11076709599695013872)
XLA Ops:
  2.6 66.3 %adafactor_step.1 = (f32[2304,768]{1,0:T(8,128)S(1)}, bf16[24,1344]{1,0:T(8,128)(2,1)S(1)}, bf16[24,960]{1,0:T(8,128)(2,1)S(1)}, f32[1,24]{1,0:T(1,128)S(1)}, f3...) custom-call(f32[1]{0:T(128)} %bitcast.23.lr_ref, f32[1]{0:T(128)} %bitcast.24.wd_ref, ...), custom_call_target="tpu_custom_call" | custom-call | tf_op jit(solution)/shard_map/adafactor_step/pallas_call | solution.py:529
  68.8 3.1 %store_outputs.1 = (f32[1344,768]{1,0:T(8,128)}, f32[960,768]{1,0:T(8,128)}, bf16[24,1344]{1,0:T(8,128)(2,1)}, bf16[24,960]{1,0:T(8,128)(2,1)}, f32[1,24]{1,0:T(...) custom-call(f32[2304,768]{1,0:T(8,128)S(1)} %get-tuple-element.23.w, ...), custom_call_target="tpu_custom_call" | custom-call | tf_op jit(solution)/shard_map/store_outputs/pallas_call | solution.py:545

commit v7 on v6

--- a/solution.py
+++ b/solution.py
@@ -21,21 +21,21 @@
 W = 24
 RING = 4
 REDUCE_SEGS = ((0, 2, 1), (2, 2, 1), (4, 5, 2))
-EARLY = 2
-GATHER_SEGS = ((0, 2, 1), (0, 2, 1), (2, 3, 2), (5, 2, 1), (7, 2, 1))
+EARLY = 3
+GATHER_SEGS = ((0, 3, 2), (0, 3, 1), (3, 4, 2), (7, 2, 1))
 BLOCKS = (0, 1, 3, 2)
 SPLIT = ((0,), (1, 3), (2,))
-GATHER_UNITS = (SPLIT, SPLIT, SPLIT, SPLIT, (None,))
+GATHER_UNITS = (SPLIT, SPLIT, SPLIT, SPLIT)
 REDUCE_UNITS = ((None,), (None,), (2, 1, 3, 0))
 RELAY_LAST = (True, False, False)
-REDUCE_PLAN = ("S0,B00,S1,B10,M00,S2,B20,B21,B22,B23,H0,M10,E00", "M20,M21,M22,M23,E10,C0,E20,E21,K0,E22,E23,a1,b10,F1,F0,F2")
-EARLY_PLAN = ("M1,N1,B11,P10,A0,B00,W1,B12,P11",)
-EARLY_PLAN_END = ("M0,N0,B01,P00,P12,W0,B02,P01",)
-GATHER_PLAN = ("A2,B20,A3,A4,P02,M2,N2,B21,P20,M3,N3,M4,N4,W2,B22,F0", "B30,B31,P21,W3,B32,W4,B40,P22,P30,P31,P32,P40,F2,F3,F4")
+REDUCE_PLAN = ("K0,a1,b10,S0,B00,S1,B10,M00,S2,B20,B21,B22,B23,M10,E00,M20,M21", "M22,M23,E10,C0,E20,E21,E22,E23,m1,n1,b11,p10,F1,F0,F2")
+EARLY_PLAN = ("A0,B00,W1,B12,P11,M0",)
+EARLY_PLAN_END = ("N0,B01,P00,W0,B02,P12,P01",)
+GATHER_PLAN = ("A2,B20,A3,P02,M2,N2,B21,P20,M3,N3,W2,B22,F0,B30,B31,P21", "W3,B32,P22,P30,P31,P32,F2,F3")
 FAR_FIRST = (2, 1, 3, 0)
 ROWS_ONE = pl.ds(0, 1)
 N_SEND = 11
-N_RECV = 59
+N_RECV = 54
 N_LOAD = 10
 
 
@@ -92,26 +92,23 @@
     loads = iter(range(N_LOAD))
 
     def remote(src, dst, dev, s, r):
-        c = pltpu.make_async_remote_copy(src_ref=src, dst_ref=dst, send_sem=send.at[s], recv_sem=recv.at[r], device_id=dev, device_id_type=MESH)
-        c.start()
+        if 0 not in src.shape:
+            pltpu.make_async_remote_copy(src_ref=src, dst_ref=dst, send_sem=send.at[s], recv_sem=recv.at[r], device_id=dev, device_id_type=MESH).start()
 
     def wait(ref, sem):
         pltpu.make_async_copy(ref, ref, sem).wait()
 
+    small = [pltpu.make_async_copy(src, dst, load_sem.at[next(loads)]) for src, dst in (
+        (h_m_in, m_in), (h_m_out, m_out), (h_r_in, r_in), (h_c_in, c_in), (h_r_out, r_out), (h_c_out, c_out))]
+    for c in small:
+        c.start()
     x_load = [next(loads) for _ in REDUCE_SEGS]
-    w_load = next(loads)
     for me in range(2):
         @pl.when(core == me)
         def _():
             for (t0, n, _), sem in zip(REDUCE_SEGS, x_load):
                 for which, lo, to, rows in spans(me, t0 * T, (t0 + n) * T):
                     pltpu.make_async_copy((g_in, g_out)[which].at[pl.ds(lo, rows)], xown.at[pl.ds(to, rows)], load_sem.at[sem]).start()
-            for which, lo, to, rows in spans(me, 0, HALF):
-                pltpu.make_async_copy((w_in, w_out)[which].at[pl.ds(lo, rows)], wown.at[pl.ds(to, rows)], load_sem.at[w_load]).start()
-    small = [pltpu.make_async_copy(src, dst, load_sem.at[next(loads)]) for src, dst in (
-        (h_m_in, m_in), (h_m_out, m_out), (h_r_in, r_in), (h_c_in, c_in), (h_r_out, r_out), (h_c_out, c_out))]
-    for c in small:
-        c.start()
 
     barrier = pltpu.get_barrier_semaphore()
     ring = ((y, *(at(x, z * RING + step(y, k), core) for k in (1, 3, 2))),
@@ -121,10 +118,20 @@
         other = lax.rem(line_me + k, 8)
         line.append(at(lax.div(other, 2), p, lax.rem(other, 2)))
     plane = [at(x, step(z, i) * RING + step(y, k), core) for i in FAR_FIRST for k in FAR_FIRST if i or k]
-    greet = [dev for _, right, left, _ in ring for dev in (right, left)] + line
+    greet = [dev for _, right, left, _ in ring for dev in (right, left)] + [at(step(x, k), p, core) for k in (2, 1, 3)] + [partner]
     for dev in greet:
         pl.semaphore_signal(barrier, inc=1, device_id=dev, device_id_type=MESH)
+
+    for c in small:
+        c.wait()
+    first = m_in[:, :HALF].astype(F32)
+    second = join_tail(m_out[...].astype(F32), m_in[:, HALF:].astype(F32), pad_a, pad_b)
+    mx[core] = jnp.where(on_first, first, second)
+    ms[...] = jnp.where(on_first, second, first)
+    fo[...] = jnp.where(on_first, c_in[:, :HALF], join_tail(r_out[...], c_in[:, HALF:], pad_c, pad_d))
     pl.semaphore_wait(barrier, len(greet))
+    m_send, m_recv = next(sends), next(recvs)
+    remote(ms, mx.at[core], partner, m_send, m_recv)
 
     swap_send = next(sends)
     swap_recv = [next(recvs) for _ in REDUCE_SEGS]
@@ -135,6 +142,13 @@
                 for which, lo, to, rows in spans(1 - me, t0 * T, (t0 + n) * T):
                     remote((g_in, g_out)[which].at[pl.ds(lo, rows)], xrecv.at[pl.ds(to, rows)], partner, swap_send, sem)
 
+    w_load = next(loads)
+    for me in range(2):
+        @pl.when(core == me)
+        def _():
+            for which, lo, to, rows in spans(me, 0, HALF):
+                pltpu.make_async_copy((w_in, w_out)[which].at[pl.ds(lo, rows)], wown.at[pl.ds(to, rows)], load_sem.at[w_load]).start()
+
     def lanes_of(seg):
         t0, n, n_a = seg
         return pl.ds(t0 * T, n_a * T), pl.ds((t0 + n_a) * T, (n - n_a) * T), pl.ds(t0 * T, n * T)
@@ -195,7 +209,8 @@
             i, right, left, r, l, f = ring_of(a)
             q = block(a, off)
             for k, lanes, dev in ((r, la, right), (l, lb, left)):
-                tbuf[(*spot(a, k, q), ALL, lanes)] += far[a, q, :, lanes]
+                if lanes.size:
+                    tbuf[(*spot(a, k, q), ALL, lanes)] += far[a, q, :, lanes]
                 remote(piece(tbuf, a, k, q, lanes), dc.at[1, a, q, :, lanes], dev, send_1, dc_sem[s][u])
 
     def rs_end(s, u):
@@ -223,7 +238,8 @@
         for a in range(2):
             i, right, left, r, l, f = ring_of(1 - a)
             for k, lanes, dev in ((r, la, right), (l, lb, left)):
-                pbuf[a, k, :, lanes] += far2[a, :, lanes]
+                if lanes.size:
+                    pbuf[a, k, :, lanes] += far2[a, :, lanes]
                 remote(pbuf.at[a, k, :, lanes], dc2.at[1, a, :, lanes], dev, send_2, dc2_sem[s])
 
     def rs_finish(s):
@@ -243,17 +259,6 @@
         wait(xown.at[rows], recv.at[swap_recv[s]])
         lax.fori_loop(t0, t0 + n, transpose_in, 0)
 
-    def prepare(_):
-        for c in small:
-            c.wait()
-        first = m_in[:, :HALF].astype(F32)
-        second = join_tail(m_out[...].astype(F32), m_in[:, HALF:].astype(F32), pad_a, pad_b)
-        mx[core] = jnp.where(on_first, first, second)
-        ms[...] = jnp.where(on_first, second, first)
-        remote(ms, mx.at[core], partner, m_send, m_recv)
-        fo[...] = jnp.where(on_first, c_in[:, :HALF], join_tail(r_out[...], c_in[:, HALF:], pad_c, pad_d))
-
-    m_send, m_recv = next(sends), next(recvs)
     send_3 = next(sends)
     a1_first, a1_rest, a1_fwd, a2_rest = ([next(recvs) for _ in GATHER_SEGS] for _ in range(4))
     a2_first = [[next(recvs) for _ in u] for u in GATHER_UNITS]
@@ -331,7 +336,7 @@
         for item in ",".join(plan).split(","):
             table[item[0]](*(int(c) for c in item[1:]))
 
-    follow(REDUCE_PLAN, dict(S=rs_load, B=rs_begin, M=rs_middle, E=rs_end, C=rs_cross, F=rs_finish, H=prepare, K=keep, a=a1_begin, b=a2_begin))
+    follow(REDUCE_PLAN, dict(S=rs_load, B=rs_begin, M=rs_middle, E=rs_end, C=rs_cross, F=rs_finish, K=keep, a=a1_begin, b=a2_begin, m=a1_middle, n=a1_near, w=a1_far, p=a2_middle))
 
     lane = lax.broadcasted_iota(jnp.int32, (1, HALF), 1)
     is_in = lane >= jnp.where(on_first, 0, F_OUT)

time: 72 us -> 70.6 us (0.981)
  Pallas kernels: 69.3 us -> 67.8 us
    pallas_call x1, Pallas kernels: 66.3 us -> 64.8 us  [call(): pl.pallas_call(kernel, name='adafactor_step', out_shape=(buf(2 * HALF, D)...]
where the time goes in v7:
time: 70.6 us; the launch traced here: 70.4 us
  Pallas kernels  67.8 us (96%)
  between operations  2.58 us (4%)
    pallas_call x1, Pallas kernels, call(): pl.pallas_call(kernel, name='adafactor_step', out_shape=(buf(2 * HALF, D)...  64.8 us
    pallas_call x1, Pallas kernels, call(): pl.pallas_call(store_kernel, name='store_outputs', out_shape=tuple((jax.S...  3.07 us

profile of v7, /device:TPU:1, one launch (start us, length us, event | category | flops | bytes accessed | tf_op | source)
XLA Modules:
  0.0 70.4 jit_solution(12531461955887448982)
XLA Ops:
  2.6 64.8 %adafactor_step.1 = (f32[2304,768]{1,0:T(8,128)S(1)}, bf16[24,1344]{1,0:T(8,128)(2,1)S(1)}, bf16[24,960]{1,0:T(8,128)(2,1)S(1)}, f32[1,24]{1,0:T(1,128)S(1)}, f3...) custom-call(f32[1]{0:T(128)} %bitcast.23.lr_ref, f32[1]{0:T(128)} %bitcast.24.wd_ref, ...), custom_call_target="tpu_custom_call" | custom-call | tf_op jit(solution)/shard_map/adafactor_step/pallas_call | solution.py:534
  67.4 3.1 %store_outputs.1 = (f32[1344,768]{1,0:T(8,128)}, f32[960,768]{1,0:T(8,128)}, bf16[24,1344]{1,0:T(8,128)(2,1)}, bf16[24,960]{1,0:T(8,128)(2,1)}, f32[1,24]{1,0:T(...) custom-call(f32[2304,768]{1,0:T(8,128)S(1)} %get-tuple-element.23.w, ...), custom_call_target="tpu_custom_call" | custom-call | tf_op jit(solution)/shard_map/store_outputs/pallas_call | solution.py:550

commit v8 on v7

--- a/solution.py
+++ b/solution.py
@@ -22,20 +22,20 @@
 RING = 4
 REDUCE_SEGS = ((0, 2, 1), (2, 2, 1), (4, 5, 2))
 EARLY = 3
-GATHER_SEGS = ((0, 3, 2), (0, 3, 1), (3, 4, 2), (7, 2, 1))
+GATHER_SEGS = ((0, 3, 2), (0, 3, 1), (3, 2, 1), (5, 2, 1), (7, 2, 1))
 BLOCKS = (0, 1, 3, 2)
 SPLIT = ((0,), (1, 3), (2,))
-GATHER_UNITS = (SPLIT, SPLIT, SPLIT, SPLIT)
+GATHER_UNITS = (SPLIT, SPLIT, SPLIT, SPLIT, SPLIT)
 REDUCE_UNITS = ((None,), (None,), (2, 1, 3, 0))
 RELAY_LAST = (True, False, False)
 REDUCE_PLAN = ("K0,a1,b10,S0,B00,S1,B10,M00,S2,B20,B21,B22,B23,M10,E00,M20,M21", "M22,M23,E10,C0,E20,E21,E22,E23,m1,n1,b11,p10,F1,F0,F2")
 EARLY_PLAN = ("A0,B00,W1,B12,P11,M0",)
 EARLY_PLAN_END = ("N0,B01,P00,W0,B02,P12,P01",)
-GATHER_PLAN = ("A2,B20,A3,P02,M2,N2,B21,P20,M3,N3,W2,B22,F0,B30,B31,P21", "W3,B32,P22,P30,P31,P32,F2,F3")
+GATHER_PLAN = ("A2,A3,B30,A4,B20,B40,P02,R0,M2,M3,N3,B31,M4,N2,B21", "W2,B22,N4,G0,W3,B32,G1,B41,W4,G2,B42,P21,P20,P22,P31", "P30,P32,P40,P41,P42,F2,F3,F4")
 FAR_FIRST = (2, 1, 3, 0)
 ROWS_ONE = pl.ds(0, 1)
 N_SEND = 11
-N_RECV = 54
+N_RECV = 61
 N_LOAD = 10
 
 
@@ -475,32 +475,38 @@
             rowpad[...] = jnp.broadcast_to(new, rowpad.shape)
             out[...] = jnp.where(on_first, rowpad[...], pltpu.roll(rowpad[...], T - W, 1))[:1, :W]
 
+    def factors(_):
+        wait(wown, load_sem.at[w_load])
+        colv[pl.ds(1, 1)] = scale
+        shifted = lax.broadcasted_iota(jnp.int32, (2 * W, T), 0) + 16 == lax.broadcasted_iota(jnp.int32, (2 * W, T), 1)
+
+        def row_factor(chip, _):
+            col = sum_of(jnp.where(shifted, qs[x * 32 + chip * 2 + core], 0.0), 1)
+            rf[chip] = jnp.broadcast_to(1.0 / jnp.sqrt(col), (2 * W, T))
+            return 0
+
+        lax.fori_loop(0, 16, row_factor, 0)
+
+    def finish_early(j):
+        if j == 0:
+            a2_end(0)
+            a2_end(1)
+        put_rows(jnp.int32(j), moments_early)
+
     def finish(s):
-        if s == 0:
-            wait(wown, load_sem.at[w_load])
-            colv[pl.ds(1, 1)] = scale
-            shifted = lax.broadcasted_iota(jnp.int32, (2 * W, T), 0) + 16 == lax.broadcasted_iota(jnp.int32, (2 * W, T), 1)
-
-            def row_factor(chip, _):
-                col = sum_of(jnp.where(shifted, qs[x * 32 + chip * 2 + core], 0.0), 1)
-                rf[chip] = jnp.broadcast_to(1.0 / jnp.sqrt(col), (2 * W, T))
-                return 0
-
-            lax.fori_loop(0, 16, row_factor, 0)
-            a2_end(1)
         if s == 2:
             state_out()
         a2_end(s)
         t0, n, _ = GATHER_SEGS[s]
 
         def tile(j, _):
-            put_rows(j, moments if s else moments_early)
+            put_rows(j, moments)
             return 0
 
         lax.fori_loop(t0, t0 + n, tile, 0)
 
     remote(mnew.at[1 - core], mrecv, partner, mo_send, mo_recv)
-    gather(GATHER_PLAN, F=finish)
+    gather(GATHER_PLAN, F=finish, R=factors, G=finish_early)
 
     wait(xown, recv.at[out_recv])
     for ref, sem in ((xown, swap_send), (ms, m_send), (tbuf.at[:3], send_1), (tbuf.at[0, :3], send_2), (fv_ref, fv_send), (rv_ref, rv_send), (q_ref, q_send),

time: 70.6 us -> 68.7 us (0.973)
  Pallas kernels: 67.8 us -> 66 us
    pallas_call x1, Pallas kernels: 64.8 us -> 62.9 us  [call(): pl.pallas_call(kernel, name='adafactor_step', out_shape=(buf(2 * HALF, D)...]
where the time goes in v8:
time: 68.7 us; the launch traced here: 68.6 us
  Pallas kernels  66 us (96%)
  between operations  2.58 us (4%)
    pallas_call x1, Pallas kernels, call(): pl.pallas_call(kernel, name='adafactor_step', out_shape=(buf(2 * HALF, D)...  62.9 us
    pallas_call x1, Pallas kernels, call(): pl.pallas_call(store_kernel, name='store_outputs', out_shape=tuple((jax.S...  3.07 us

profile of v8, /device:TPU:1, one launch (start us, length us, event | category | flops | bytes accessed | tf_op | source)
XLA Modules:
  0.0 68.6 jit_solution(15542843181365697937)
XLA Ops:
  2.6 62.9 %adafactor_step.1 = (f32[2304,768]{1,0:T(8,128)S(1)}, bf16[24,1344]{1,0:T(8,128)(2,1)S(1)}, bf16[24,960]{1,0:T(8,128)(2,1)S(1)}, f32[1,24]{1,0:T(1,128)S(1)}, f3...) custom-call(f32[1]{0:T(128)} %bitcast.23.lr_ref, f32[1]{0:T(128)} %bitcast.24.wd_ref, ...), custom_call_target="tpu_custom_call" | custom-call | tf_op jit(solution)/shard_map/adafactor_step/pallas_call | solution.py:540
  65.5 3.1 %store_outputs.1 = (f32[1344,768]{1,0:T(8,128)}, f32[960,768]{1,0:T(8,128)}, bf16[24,1344]{1,0:T(8,128)(2,1)}, bf16[24,960]{1,0:T(8,128)(2,1)}, f32[1,24]{1,0:T(...) custom-call(f32[2304,768]{1,0:T(8,128)S(1)} %get-tuple-element.23.w, ...), custom_call_target="tpu_custom_call" | custom-call | tf_op jit(solution)/shard_map/store_outputs/pallas_call | solution.py:556

commit v9 on v8

--- a/solution.py
+++ b/solution.py
@@ -261,6 +261,7 @@
 
     send_3 = next(sends)
     a1_first, a1_rest, a1_fwd, a2_rest = ([next(recvs) for _ in GATHER_SEGS] for _ in range(4))
+    a1_rest[3] = a1_first[3]
     a2_first = [[next(recvs) for _ in u] for u in GATHER_UNITS]
 
     def swap_around(ref, ring_a, s, first, rest):
@@ -305,11 +306,14 @@
         swap_around(two_ref(s, u), same, s, a2_first[s][u], a2_rest[s])
 
     def a1_middle(s):
-        wait(far2.at[:, :, lanes_of(GATHER_SEGS[s])[-1]], recv.at[a1_first[s]])
+        full = lanes_of(GATHER_SEGS[s])[-1]
+        both = a1_rest[s] == a1_first[s]
+        wait(dc2.at[:2, :, :, full] if both else far2.at[:, :, full], recv.at[a1_first[s]])
         pass_on(one_ref(s), other, s, a1_fwd[s])
 
     def a1_near(s):
-        wait(far2.at[:, :, lanes_of(GATHER_SEGS[s])[-1]], recv.at[a1_rest[s]])
+        if a1_rest[s] != a1_first[s]:
+            wait(far2.at[:, :, lanes_of(GATHER_SEGS[s])[-1]], recv.at[a1_rest[s]])
 
     def a1_far(s):
         wait(far2.at[:, :, lanes_of(GATHER_SEGS[s])[-1]], recv.at[a1_fwd[s]])
@@ -515,14 +519,15 @@
 
 
 def store_kernel(w, m_in, m_out, r_in, c_in, r_out, c_out, o_w_in, o_w_out, o_m_in, o_m_out, o_r_in, o_c_in, o_r_out, o_c_out, sem):
-    pairs = [(w.at[pl.ds(src + k * rows, rows)], out.at[pl.ds(dst + k * rows, rows)]) for src, out, dst, rows, count in (
-        (0, o_w_in, 0, TAIL, 6), (HALF, o_w_out, 0, TAIL, 5), (HALF + F_OUT, o_w_in, HALF, TAIL, 1)) for k in range(count)]
-    pairs += [(m_in, o_m_in), (m_out, o_m_out), (r_in, o_r_in), (c_in, o_c_in), (r_out, o_r_out), (c_out, o_c_out)]
-    work = [pltpu.make_async_copy(src, dst, sem.at[n]) for n, (src, dst) in enumerate(pairs)]
-    for c in work:
+    work = [pltpu.make_async_copy(w.at[pl.ds(src, rows)], out.at[pl.ds(dst, rows)], sem.at[0]) for src, out, dst, rows in (
+        (0, o_w_in, 0, HALF), (HALF, o_w_out, 0, F_OUT), (HALF + F_OUT, o_w_in, HALF, TAIL))]
+    few = [pltpu.make_async_copy(src, dst, sem.at[n + 1]) for n, (src, dst) in enumerate((
+        (m_in, o_m_in), (m_out, o_m_out), (r_in, o_r_in), (c_in, o_c_in), (r_out, o_r_out), (c_out, o_c_out)))]
+    for c in work + few:
         c.start()
-    for c in work:
+    for c in few:
         c.wait()
+    pltpu.make_async_copy(w, w, sem.at[0]).wait()
 
 
 def call(*args):
@@ -559,7 +564,7 @@
         out_shape=tuple(jax.ShapeDtypeStruct(*a) for a in (((F_IN, D), F32), ((F_OUT, D), F32), *small)),
         in_specs=[vmem] * (1 + len(small)),
         out_specs=(hbm,) * (2 + len(small)),
-        scratch_shapes=[pltpu.SemaphoreType.DMA((18,))],
+        scratch_shapes=[pltpu.SemaphoreType.DMA((7,))],
         compiler_params=pltpu.CompilerParams(vmem_limit_bytes=16 << 20),
     )(*held)
 

time: 68.7 us -> 68.6 us (level)
  no operation moved by 1% of the time
where the time goes in v9:
time: 68.6 us; the launch traced here: 68.5 us
  Pallas kernels  65.9 us (96%)
  between operations  2.58 us (4%)
    pallas_call x1, Pallas kernels, call(): pl.pallas_call(kernel, name='adafactor_step', out_shape=(buf(2 * HALF, D)...  62.9 us
    pallas_call x1, Pallas kernels, call(): pl.pallas_call(store_kernel, name='store_outputs', out_shape=tuple((jax.S...  3.03 us

profile of v9, /device:TPU:1, one launch (start us, length us, event | category | flops | bytes accessed | tf_op | source)
XLA Modules:
  0.0 68.5 jit_solution(15658602423631407585)
XLA Ops:
  2.6 62.9 %adafactor_step.1 = (f32[2304,768]{1,0:T(8,128)S(1)}, bf16[24,1344]{1,0:T(8,128)(2,1)S(1)}, bf16[24,960]{1,0:T(8,128)(2,1)S(1)}, f32[1,24]{1,0:T(1,128)S(1)}, f3...) custom-call(f32[1]{0:T(128)} %bitcast.23.lr_ref, f32[1]{0:T(128)} %bitcast.24.wd_ref, ...), custom_call_target="tpu_custom_call" | custom-call | tf_op jit(solution)/shard_map/adafactor_step/pallas_call | solution.py:545
  65.5 3.0 %store_outputs.1 = (f32[1344,768]{1,0:T(8,128)}, f32[960,768]{1,0:T(8,128)}, bf16[24,1344]{1,0:T(8,128)(2,1)}, bf16[24,960]{1,0:T(8,128)(2,1)}, f32[1,24]{1,0:T(...) custom-call(f32[2304,768]{1,0:T(8,128)S(1)} %get-tuple-element.23.w, ...), custom_call_target="tpu_custom_call" | custom-call | tf_op jit(solution)/shard_map/store_outputs/pallas_call | solution.py:561
